TPU v7x, 32 devices: a whole 2x2x4 slice. The times are simulated.
32 devices in a mesh: pts: 16 (over z, x, core), tau: 2 (over y).
Axes of the slice: x: 2, y: 2, z: 4, core: 2. Of those that a mesh axis runs over, the one named last changes fastest.
Arguments:
- occupied_values: float32 [256, 512], P(('pts', 'tau')), may hold values from -2.5 to 2.5
- virtual_values: float32 [256, 1536], P(('pts', 'tau')), may hold values from -1.75 to 1.75
- occupied_energy: float32 [512], replicated, may hold values from -1 to -0.05
- virtual_energy: float32 [1536], replicated, may hold values from 0.05 to 2
- tau_points: float32 [2], replicated, may hold values from 0.1 to 3
- tau_weights: float32 [2], replicated, may hold values from 0.2 to 1
- frequencies: float32 [2], replicated, may hold values from 0.1 to 3
- pair_live: int32 [16, 16], P('pts'), may hold values from 0 to 1, as said below
Outputs:
- polarizability: float32 [2, 256, 2, 128], P(None, 'pts', 'tau')
Inputs may be any that keep to these rules, and one draw needn't show every extreme that they name: `pair_live`: 1 marks a block pair that is formed, 0 one that is left out; every diagonal entry is 1.
All inputs are finite; a program needn't handle non-finite values.
Results may differ from a plain program's by a relative error of at most 0.000076.
Values sent between devices are 32-bit elements; how exact they have to be, the bound alone decides.
No kernel may reach another device: no remote copies, remote signals or barrier semaphores. Data moves between devices by JAX's collectives and lax.ppermute only.
A program may use at most 64 MiB of HBM per device.

v0:
```python
import jax
import jax.numpy as jnp
from jax import lax
from jax.sharding import PartitionSpec as P


def on_device(
    occupied_values,
    virtual_values,
    occupied_energy,
    virtual_energy,
    tau_points,
    tau_weights,
    frequencies,
    pair_live,
):
    highest = lax.Precision.HIGHEST
    device_pts = occupied_values.shape[0]
    row_occupied, row_virtual = (
        lax.all_gather(occupied_values, "tau", axis=0, tiled=True),
        lax.all_gather(virtual_values, "tau", axis=0, tiled=True),
    )
    occupied_scaled = (
        row_occupied[None] * jnp.exp(occupied_energy[None, :] * tau_points[:, None])[:, None, :]
    )
    virtual_scaled = (
        row_virtual[None] * jnp.exp(-virtual_energy[None, :] * tau_points[:, None])[:, None, :]
    )
    column_mask = jnp.repeat(pair_live[0].astype(jnp.float32), device_pts)
    column_occupied, column_virtual = (
        lax.all_gather(occupied_values, "pts", axis=0, tiled=True),
        lax.all_gather(virtual_values, "pts", axis=0, tiled=True),
    )
    green_occupied = jnp.einsum(
        "trw,nw->trn",
        occupied_scaled,
        column_occupied,
        precision=highest,
        preferred_element_type=jnp.float32,
    )
    green_virtual = jnp.einsum(
        "trw,nw->trn",
        virtual_scaled,
        column_virtual,
        precision=highest,
        preferred_element_type=jnp.float32,
    )
    chi_time = -(green_occupied * green_virtual) * column_mask[None, None, :]
    mixing = 2.0 * tau_weights[None, :] * jnp.cos(frequencies[:, None] * tau_points[None, :])
    chi_freq = jnp.einsum("kt,trn->krn", mixing, chi_time, precision=highest)
    return chi_freq[:, :, None, :]


def solution(mesh):
    return jax.shard_map(
        on_device,
        mesh=mesh,
        in_specs=(
            P(("pts", "tau"), None),
            P(("pts", "tau"), None),
            P(),
            P(),
            P(),
            P(),
            P(),
            P("pts", None),
        ),
        out_specs=P(None, "pts", "tau", None),
        check_vma=False,
    )
```

profile of v0, /device:TPU:0, one launch (start us, length us, event | category | flops | bytes accessed | tf_op | source)
XLA Modules:
  0.0 57.8 jit_solution(11849358803733473706)
XLA Ops:
  0.0 0.0 copy-start
  0.0 25.8 %all_gather.15 = f32[128,1536]{1,0:T(8,128)S(1)} all-gather(f32[8,1536]{1,0:T(8,128)} %param.9), channel_id=1, replica_groups=mesh['pts'=16,'tau'=2] {'pts'}, dimensions={0}, use_global_device_ids=true | all-gather | bytes 835584 | tf_op jit(solution)/shard_map/all_gather | solution.py:32
  25.8 0.0 copy-done
  25.8 0.0 copy-start.2
  25.8 4.9 %all_gather.14 = f32[16,1536]{1,0:T(8,128)S(1)} all-gather(f32[8,1536]{1,0:T(8,128)S(1)} %copy-done), channel_id=1, replica_groups=mesh['pts'=16,'tau'=2] {'tau'}, dimensions={0}, use_global_device_ids=true | all-gather | bytes 147456 | tf_op jit(solution)/shard_map/all_gather | solution.py:21
  30.7 0.0 copy-done.2
  30.7 0.0 copy-start.4
  30.7 0.7 %copy-done.4 = f32[2]{0:T(128)S(1)} copy-done((f32[2]{0:T(128)S(1)}, f32[2]{0:T(128)}, u32[]{:S(2)}) %copy-start.4) | copy-done | bytes 32
  31.4 0.1 multiply_exponential_fusion
  31.4 0.0 copy-start.1
  31.5 0.9 %fusion = f32[2,16,128]{2,1,0:T(8,128)S(1)} fusion(f32[128,1536]{1,0:T(8,128)S(1)} %all_gather.15, f32[2,1536]{1,0:T(2,128)S(1)} %multiply_exponential_fusion, f32[16,1536]{1,0:T(8,128)S(1)} %all_gather.14), kind=kOutput, calls=%fused_computation.1 | convolution fusion | flops 75546624 | bytes 913408 | tf_op jit(solution)/shard_map/trw,nw->trn/dot_general | solution.py:41
  32.3 0.0 copy-done.1
  32.3 17.8 %all_gather.13 = f32[128,512]{1,0:T(8,128)S(1)} all-gather(f32[8,512]{1,0:T(8,128)S(1)} %copy-done.1), channel_id=1, replica_groups=mesh['pts'=16,'tau'=2] {'pts'}, dimensions={0}, use_global_device_ids=true | all-gather | bytes 278528 | tf_op jit(solution)/shard_map/all_gather | solution.py:31
  50.2 4.5 %all_gather.12 = f32[16,512]{1,0:T(8,128)S(1)} all-gather(f32[8,512]{1,0:T(8,128)S(1)} %copy-done.1), channel_id=1, replica_groups=mesh['pts'=16,'tau'=2] {'tau'}, dimensions={0}, use_global_device_ids=true | all-gather | bytes 49152 | tf_op jit(solution)/shard_map/all_gather | solution.py:20
  54.7 0.0 copy-done.3
  54.7 0.1 multiply_exponential_fusion.1
  54.8 0.4 fusion.2
  55.2 0.3 copy-done.5
  55.5 0.1 broadcast_in_dim.4
  55.5 0.1 mul.117
  55.6 0.6 copy-done.6
  56.2 0.7 %copy-done.7 = f32[2]{0:T(128)S(1)} copy-done((f32[2]{0:T(128)S(1)}, f32[2]{0:T(128)}, u32[]{:S(2)}) %copy-start.7) | copy-done | bytes 32
  56.8 0.3 convolution_bitcast_fusion
  57.2 0.6 %copy.10 = f32[2,16,1,128]{3,2,1,0:T(1,128)} copy(f32[2,16,1,128]{3,0,1,2:T(2,128)S(1)} %convolution_bitcast_fusion) | data formatting | bytes 32768 | tf_op jit(solution)/shard_map/broadcast_in_dim | solution.py:51
  (7 shorter events, 0.0 us)
Async XLA Ops:
  0.0 25.8 %copy-start = (f32[8,1536]{1,0:T(8,128)S(1)}, f32[8,1536]{1,0:T(8,128)}, u32[]{:S(2)}) copy-start(f32[8,1536]{1,0:T(8,128)} %param.9) | copy-start | bytes 147460
  25.8 4.9 %copy-start.2 = (f32[1536]{0:T(1024)S(1)}, f32[1536]{0:T(1024)}, u32[]{:S(2)}) copy-start(f32[1536]{0:T(1024)} %param.11) | copy-start | bytes 18436
  30.7 0.7 %copy-start.4 = (f32[2]{0:T(128)S(1)}, f32[2]{0:T(128)}, u32[]{:S(2)}) copy-start(f32[2]{0:T(128)} %param.12) | copy-start | bytes 28
  31.4 0.9 %copy-start.1 = (f32[8,512]{1,0:T(8,128)S(1)}, f32[8,512]{1,0:T(8,128)}, u32[]{:S(2)}) copy-start(f32[8,512]{1,0:T(8,128)} %param.8) | copy-start | bytes 49156
  50.2 4.5 %copy-start.3 = (f32[512]{0:T(512)S(1)}, f32[512]{0:T(512)}, u32[]{:S(2)}) copy-start(f32[512]{0:T(512)} %param.10) | copy-start | bytes 6148
  54.8 0.7 %copy-start.5 = (s32[1,16]{1,0:T(1,128)S(1)}, s32[1,16]{1,0:T(1,128)}, u32[]{:S(2)}) copy-start(s32[1,16]{1,0:T(1,128)} %param.15) | copy-start | bytes 196
  55.5 0.7 %copy-start.6 = (f32[2]{0:T(128)S(1)}, f32[2]{0:T(128)}, u32[]{:S(2)}) copy-start(f32[2]{0:T(128)} %param.13) | copy-start | bytes 28
  56.2 0.7 %copy-start.7 = (f32[2]{0:T(128)S(1)}, f32[2]{0:T(128)}, u32[]{:S(2)}) copy-start(f32[2]{0:T(128)} %param.14) | copy-start | bytes 28
where the time goes:
time: 58 us; the launch traced here: 57.8 us
  blocking collectives  53.1 us (92%)
  local copies, waits for them, and re-layouts  2.96 us (5%)
  matrix products  1.53 us (3%)
    all_gather x1, blocking collectives, on_device(): lax.all_gather(virtual_values, 'pts', axis=0, tiled=True)  25.8 us
    all_gather x1, blocking collectives, on_device(): lax.all_gather(occupied_values, 'pts', axis=0, tiled=True)  17.8 us
    all_gather x1, blocking collectives, on_device(): lax.all_gather(virtual_values, 'tau', axis=0, tiled=True)  4.88 us
    all_gather x1, blocking collectives, on_device(): lax.all_gather(occupied_values, 'tau', axis=0, tiled=True)  4.53 us
    unnamed x16, local copies, waits for them, and re-layouts  2.17 us

commit v1 on v0

v1 whole, which is shorter than its diff:
```python
import functools

import jax
import jax.numpy as jnp
from jax import lax
from jax.sharding import PartitionSpec as P

AXES = ("pts", "tau")
DIRECT = 4


def layout(mesh):
    points, groups = mesh.shape["pts"], mesh.shape["tau"]
    cores = 2 if points % 2 == 0 else 1
    pairs = 2 if points % (2 * cores) == 0 else 1
    return points // (pairs * cores), pairs, cores, groups


def gather(mesh, dim, block):
    sizes = layout(mesh)
    strides = (sizes[1] * sizes[2] * sizes[3], sizes[2] * sizes[3], sizes[3], 1)
    size, stride, n = sizes[dim], strides[dim], sizes[0] * strides[0]
    mine = (lax.axis_index(AXES) // stride) % size
    if size <= DIRECT and size & (size - 1) == 0:
        blocks, coords = [block], [mine]
        for step in range(size - 1, 0, -1):
            pairs = [(i, i + (((i // stride) % size) ^ step) * stride - ((i // stride) % size) * stride) for i in range(n)]
            blocks.append(lax.ppermute(block, AXES, pairs))
            coords.append(mine ^ step)
        return blocks, coords
    firsts = [i for i in range(n) if (i // stride) % size == 0]
    members = [[i + k * stride for k in range(size)] for i in firsts]
    every = lax.all_gather(block, AXES, axis=0, axis_index_groups=members)
    order = [(mine + k) % size for k in range(size)]
    return [every[k] for k in order], order


def on_device(
    mesh,
    occupied_values,
    virtual_values,
    occupied_energy,
    virtual_energy,
    tau_points,
    tau_weights,
    frequencies,
    pair_live,
):
    highest = lax.Precision.HIGHEST
    device_pts, n_occupied = occupied_values.shape
    far, pairs, cores, groups = layout(mesh)
    me = lax.axis_index("pts")
    pair = (me // cores) % pairs

    own = jnp.concatenate([occupied_values, virtual_values], axis=1)
    far_blocks, far_at = gather(mesh, 0, own)
    row_blocks, row_at = gather(mesh, 3, own)
    rows = jnp.concatenate(row_blocks, axis=0)
    row_sets, _ = gather(mesh, 1, rows)
    column_sets, core_at = gather(mesh, 2, jnp.concatenate(far_blocks, axis=0))
    columns = jnp.concatenate(column_sets, axis=0)

    occupied_decay = jnp.exp(occupied_energy[None, :] * tau_points[:, None])[:, None, :]
    virtual_decay = jnp.exp(-virtual_energy[None, :] * tau_points[:, None])[:, None, :]
    mixing = 2.0 * tau_weights[None, :] * jnp.cos(frequencies[:, None] * tau_points[None, :])

    def chi_of(part):
        green_occupied = jnp.einsum(
            "trw,nw->trn", part[None, :, :n_occupied] * occupied_decay, columns[:, :n_occupied], precision=highest
        )
        green_virtual = jnp.einsum(
            "trw,nw->trn", part[None, :, n_occupied:] * virtual_decay, columns[:, n_occupied:], precision=highest
        )
        return jnp.einsum("kt,trn->krn", mixing, -(green_occupied * green_virtual), precision=highest)

    n = far * pairs * cores * groups
    results, result_at = [chi_of(rows)], [pair]
    for step in range(1, pairs):
        swap = cores * groups * step
        there = chi_of(row_sets[step])
        results.append(lax.ppermute(there, AXES, [(i, i ^ swap) for i in range(n)]))
        result_at.append(pair ^ step)

    blocks = jnp.stack(
        [(f * pairs + x) * cores + c for x in result_at for c in core_at for f in far_at]
    )
    place = (blocks[:, None] * device_pts + jnp.arange(device_pts)[None, :]).reshape(-1)
    spread = (place[:, None] == jnp.arange(place.shape[0])[None, :]).astype(jnp.float32)
    chi = jnp.einsum("krm,mn->krn", jnp.concatenate(results, axis=-1), spread, precision=highest)
    row_place = (jnp.stack(row_at)[:, None] * device_pts + jnp.arange(device_pts)[None, :]).reshape(-1)
    row_spread = (row_place[None, :] == jnp.arange(row_place.shape[0])[:, None]).astype(jnp.float32)
    chi = jnp.einsum("sr,krn->ksn", row_spread, chi, precision=highest)
    column_mask = jnp.repeat(pair_live[0].astype(jnp.float32), device_pts)
    return (chi * column_mask[None, None, :])[:, :, None, :]


def solution(mesh):
    return jax.shard_map(
        functools.partial(on_device, mesh),
        mesh=mesh,
        in_specs=(P(AXES, None), P(AXES, None), P(), P(), P(), P(), P(), P("pts", None)),
        out_specs=P(None, "pts", "tau", None),
        check_vma=False,
    )
```

time: 58 us -> 26.6 us (0.46)
  blocking collectives: 53.1 us -> 0 us
  starting transfers between devices: 0 us -> 10.6 us
  waiting for transfers between devices: 0 us -> 5.58 us
  local copies, waits for them, and re-layouts: 2.96 us -> 6.45 us
  matrix products: 1.53 us -> 2.92 us
    all_gather x4 -> x0, blocking collectives: 53.1 us -> none  [the longest x1 25.8 us: on_device(): lax.all_gather(virtual_values, 'pts', axis=0, tiled=True)]
    ppermute x0 -> x7, starting transfers between devices: none -> 10.6 us  [the longest x6 9.08 us: gather(): blocks.append(lax.ppermute(block, AXES, pairs))]
    ppermute x0 -> x7, waiting for transfers between devices: none -> 5.58 us  [the longest x6 4.35 us: gather(): blocks.append(lax.ppermute(block, AXES, pairs))]
    unnamed x16 -> x20, local copies, waits for them, and re-layouts: 2.17 us -> 4.82 us
    dot_general x3 -> x8, matrix products: 1.53 us -> 2.92 us  [the longest x2 0.88 us: chi_of(): jnp.einsum('trw,nw->trn', part[None, :, n_occupied:] * virtual_decay, col...]
    slice x0 -> x4, local copies, waits for them, and re-layouts: none -> 1.18 us  [the longest x2 0.87 us: chi_of(): part[None, :, n_occupied:] * virtual_decay]
    broadcast_in_dim x1 -> x0, local copies, waits for them, and re-layouts: 0.62 us -> none  [on_device(): return chi_freq[:, :, None, :]]
  transfers between devices with their start and end apart: 0 -> 7, of which waited for: 0 -> 2; matrix products, arithmetic and copies ran while one was open for 0% -> 7% of each run, Pallas kernels for 0% -> 0%
where the time goes in v1:
time: 26.6 us; the launch traced here: 26.2 us
  starting transfers between devices  10.6 us (40%)
  local copies, waits for them, and re-layouts  6.45 us (24%)
  waiting for transfers between devices  5.58 us (21%)
  matrix products  2.92 us (11%)
  other arithmetic  0.43 us (2%)
    ppermute x6, starting transfers between devices, gather(): blocks.append(lax.ppermute(block, AXES, pairs))  9.08 us
    unnamed x20, local copies, waits for them, and re-layouts  4.82 us
    ppermute x6, waiting for transfers between devices, gather(): blocks.append(lax.ppermute(block, AXES, pairs))  4.35 us
    ppermute x1, starting transfers between devices, on_device(): results.append(lax.ppermute(there, AXES, [(i, i ^ swap) for i in range(n)]))  1.56 us
    ppermute x1, waiting for transfers between devices, on_device(): results.append(lax.ppermute(there, AXES, [(i, i ^ swap) for i in range(n)]))  1.24 us
    dot_general x2, matrix products, chi_of(): jnp.einsum('trw,nw->trn', part[None, :, n_occupied:] * virtual_decay, col...  0.88 us
    slice x2, local copies, waits for them, and re-layouts, chi_of(): part[None, :, n_occupied:] * virtual_decay  0.87 us
    dot_general x1, matrix products, on_device(): chi = jnp.einsum('sr,krn->ksn', row_spread, chi, precision=highest)  0.77 us
  transfers between devices with their start and end apart: 7, of which 2 were waited for; matrix products, arithmetic and copies ran while one was open for 7% of the time, Pallas kernels for 0%

profile of v1, /device:TPU:0, one launch (start us, length us, event | category | flops | bytes accessed | tf_op | source)
XLA Modules:
  0.0 26.2 jit_solution(10198788186378070293)
XLA Ops:
  0.0 0.7 %constant_dynamic-update-slice_fusion.1 = (f32[8,2048]{1,0:T(8,128)S(1)}, f32[64,2048]{1,0:T(8,128)S(1)}) fusion(f32[8,512]{1,0:T(8,128)} %param.8), kind=kLoop, calls=%fused_computation.34 | loop fusion | bytes 49152
  0.8 5.1 %collective-permute-start.1 = (f32[8,2048]{1,0:T(8,128)S(1)}, f32[8,2048]{1,0:T(8,128)S(1)}, u32[]{:S(2)}, u32[]{:S(2)}) collective-permute-start(f32[8,2048]{1,0:T(8,128)S(1)} %get-tuple-element.5), channel_id=1, source_target_pairs={{0,24},{1,25},{2,26},{3,27},{4,28},{5,29},{6,30},{7,31},{8,16},{9,... | collective-permute-start | bytes 196616 | tf_op jit(solution)/shard_map/ppermute | solution.py:28
  6.0 0.6 %collective-permute-start.3 = (f32[8,2048]{1,0:T(8,128)S(1)}, f32[8,2048]{1,0:T(8,128)S(1)}, u32[]{:S(2)}, u32[]{:S(2)}) collective-permute-start(f32[8,2048]{1,0:T(8,128)S(1)} %get-tuple-element.5), channel_id=1, source_target_pairs={{0,8},{1,9},{2,10},{3,11},{4,12},{5,13},{6,14},{7,15},{8,0},{9,1},... | collective-permute-start | bytes 196616 | tf_op jit(solution)/shard_map/ppermute | solution.py:28
  6.6 1.7 %collective-permute-start = (f32[8,2048]{1,0:T(8,128)S(1)}, f32[8,2048]{1,0:T(8,128)S(1)}, u32[]{:S(2)}, u32[]{:S(2)}) collective-permute-start(f32[8,2048]{1,0:T(8,128)S(1)} %get-tuple-element.5), channel_id=1, source_target_pairs={{0,1},{1,0},{2,3},{3,2},{4,5},{5,4},{6,7},{7,6},{8,9},{9,8},{10,11... | collective-permute-start | bytes 196616 | tf_op jit(solution)/shard_map/ppermute | solution.py:28
  8.5 0.5 %copy-done.2 = f32[1536]{0:T(1024)S(1)} copy-done((f32[1536]{0:T(1024)S(1)}, f32[1536]{0:T(1024)}, u32[]{:S(2)}) %copy-start.2) | copy-done | bytes 6168
  9.0 0.7 %copy-done.4 = f32[2]{0:T(128)S(1)} copy-done((f32[2]{0:T(128)S(1)}, f32[2]{0:T(128)}, u32[]{:S(2)}) %copy-start.4) | copy-done | bytes 32
  9.7 0.6 %copy-done.3 = f32[512]{0:T(512)S(1)} copy-done((f32[512]{0:T(512)S(1)}, f32[512]{0:T(512)}, u32[]{:S(2)}) %copy-start.3) | copy-done | bytes 2072
  10.4 0.6 %copy-done.5 = f32[2]{0:T(128)S(1)} copy-done((f32[2]{0:T(128)S(1)}, f32[2]{0:T(128)}, u32[]{:S(2)}) %copy-start.5) | copy-done | bytes 32
  11.1 0.6 %copy-done.6 = s32[1,16]{1,0:T(1,128)S(1)} copy-done((s32[1,16]{1,0:T(1,128)S(1)}, s32[1,16]{1,0:T(1,128)}, u32[]{:S(2)}) %copy-start.6) | copy-done | bytes 88
  12.2 1.6 %collective-permute-start.5 = (f32[16,2048]{1,0:T(8,128)S(1)}, f32[16,2048]{1,0:T(8,128)S(1)}, u32[]{:S(2)}, u32[]{:S(2)}) collective-permute-start(f32[16,2048]{1,0:T(8,128)S(1)} %pad_maximum_fusion.1), channel_id=1, source_target_pairs={{0,4},{1,5},{2,6},{3,7},{4,0},{5,1},{6,2},{7,3},{8,12},{9,13},{10,... | collective-permute-start | bytes 393224 | tf_op jit(solution)/shard_map/ppermute | solution.py:28
  13.8 4.3 %collective-permute-done.5 = f32[16,2048]{1,0:T(8,128)S(1)} collective-permute-done((f32[16,2048]{1,0:T(8,128)S(1)}, f32[16,2048]{1,0:T(8,128)S(1)}, u32[]{:S(2)}, u32[]{:S(2)}) %collective-permute-start.5) | collective-permute-done | bytes 131104 | tf_op jit(solution)/shard_map/ppermute | solution.py:28
  18.1 0.6 %copy-done = f32[16,2048]{1,0:T(8,128)} copy-done((f32[16,2048]{1,0:T(8,128)}, f32[16,2048]{1,0:T(8,128)S(1)}, u32[]{:S(2)}) %copy-start) | copy-done | bytes 131096
  18.8 0.9 %slice-done = f32[16,1536]{1,0:T(8,128)S(1)} async-done(((f32[16,2048]{1,0:T(8,128)}), f32[16,1536]{1,0:T(8,128)S(1)}, s32[]{:S(2)}) %slice-start) | async-done | bytes 98328 | tf_op jit(solution)/shard_map/slice | solution.py:72
  19.7 0.4 %fusion.2 = f32[2,16,64]{2,1,0:T(8,128)S(1)} fusion(f32[64,2048]{1,0:T(8,128)S(1)} %constant_dynamic-update-slice_fusion.2, f32[16,1536]{1,0:T(8,128)S(1)} %slice-done, f32[2,1536]{1,0:T(2,128)S(1)} %multiply_exponential_fusion), kind=kOutput, calls=%fused_computation.6 | convolution fusion | flops 37797888 | bytes 512000 | tf_op jit(solution)/shard_map/trw,nw->trn/dot_general | solution.py:71
  20.1 0.3 %slice-done.1 = f32[16,512]{1,0:T(8,128)S(1)} async-done(((f32[16,2048]{1,0:T(8,128)}), f32[16,512]{1,0:T(8,128)S(1)}, s32[]{:S(2)}) %slice-start.1) | async-done | bytes 32792 | tf_op jit(solution)/shard_map/slice | solution.py:69
  20.4 0.2 fusion
  20.7 0.4 %copy-done.7 = f32[2]{0:T(128)S(1)} copy-done((f32[2]{0:T(128)S(1)}, f32[2]{0:T(128)}, u32[]{:S(2)}) %copy-start.7) | copy-done | bytes 32
  21.1 0.3 %fusion.25 = f32[2,16,64]{2,0,1:T(2,128)S(1)} fusion(f32[2,16,64]{2,1,0:T(8,128)S(1)} %fusion, f32[2]{0:T(128)S(1)} %copy-done.4, f32[2]{0:T(128)S(1)} %broadcast_multiply_fusion.1, f32[2]{0:T(128)S(1)} %copy-done.7), kind=kOutput, calls=%fused_computation.44 | convolution fusion | flops 49160 | bytes 16408 | tf_op jit(solution)/shard_map/kt,trn->krn/dot_general | solution.py:74
  21.4 1.6 %collective-permute-start.6 = (f32[2,16,64]{2,1,0:T(8,128)S(1)}, f32[2,16,64]{2,1,0:T(8,128)S(1)}, u32[]{:S(2)}, u32[]{:S(2)}) collective-permute-start(f32[2,16,64]{2,1,0:T(8,128)S(1)} %copy.14), channel_id=1, source_target_pairs={{0,4},{1,5},{2,6},{3,7},{4,0},{5,1},{6,2},{7,3},{8,12},{9,13},{10,... | collective-permute-start | bytes 24584 | tf_op jit(solution)/shard_map/ppermute | solution.py:81
  23.0 0.4 %fusion.3 = f32[2,16,64]{2,1,0:T(8,128)S(1)} fusion(f32[64,2048]{1,0:T(8,128)S(1)} %constant_dynamic-update-slice_fusion.2, f32[2,1536]{1,0:T(2,128)S(1)} %multiply_exponential_fusion, f32[16,1536]{1,0:T(8,128)S(1)} %fusion.6), kind=kOutput, calls=%fused_computation.7 | convolution fusion | flops 37797888 | bytes 512000 | tf_op jit(solution)/shard_map/trw,nw->trn/dot_general | solution.py:71
  23.4 0.2 fusion.1
  23.7 0.3 %fusion.27 = f32[2,16,64]{2,0,1:T(2,128)S(1)} fusion(f32[2,16,64]{2,1,0:T(8,128)S(1)} %fusion.1, f32[2]{0:T(128)S(1)} %copy-done.4, f32[2]{0:T(128)S(1)} %broadcast_multiply_fusion.1, f32[2]{0:T(128)S(1)} %copy-done.7), kind=kOutput, calls=%fused_computation.46 | convolution fusion | flops 49160 | bytes 16408 | tf_op jit(solution)/shard_map/kt,trn->krn/dot_general | solution.py:74
  24.0 1.2 %collective-permute-done.6 = f32[2,16,64]{2,1,0:T(8,128)S(1)} collective-permute-done((f32[2,16,64]{2,1,0:T(8,128)S(1)}, f32[2,16,64]{2,1,0:T(8,128)S(1)}, u32[]{:S(2)}, u32[]{:S(2)}) %collective-permute-start.6) | collective-permute-done | bytes 8224 | tf_op jit(solution)/shard_map/ppermute | solution.py:81
  25.4 0.8 %convolution_multiply_fusion = f32[2,128,16]{1,2,0:T(8,128)} fusion(f32[2,16,128]{2,1,0:T(8,128)S(1)} %fusion.14, f32[128]{0:T(128)S(1)} %mul.242, s32[16]{0:T(128)S(1)} %add.178), kind=kOutput, calls=%fused_computation | convolution fusion | flops 790784 | bytes 33344 | tf_op jit(solution)/shard_map/sr,krn->ksn/dot_general | solution.py:92
  (44 shorter events, 1.3 us)
Async XLA Ops:
  0.0 0.8 %copy-start.1 = (f32[8,1536]{1,0:T(8,128)S(1)}, f32[8,1536]{1,0:T(8,128)}, u32[]{:S(2)}) copy-start(f32[8,1536]{1,0:T(8,128)} %param.9) | copy-start | bytes 147460
  0.8 11.2 %collective-permute-start.1 = (f32[8,2048]{1,0:T(8,128)S(1)}, f32[8,2048]{1,0:T(8,128)S(1)}, u32[]{:S(2)}, u32[]{:S(2)}) collective-permute-start(f32[8,2048]{1,0:T(8,128)S(1)} %get-tuple-element.5), channel_id=1, source_target_pairs={{0,24},{1,25},{2,26},{3,27},{4,28},{5,29},{6,30},{7,31},{8,16},{9,... | collective-permute-start | bytes 196616 | tf_op jit(solution)/shard_map/ppermute | solution.py:28
  6.0 6.1 %collective-permute-start.2 = (f32[8,2048]{1,0:T(8,128)S(1)}, f32[8,2048]{1,0:T(8,128)S(1)}, u32[]{:S(2)}, u32[]{:S(2)}) collective-permute-start(f32[8,2048]{1,0:T(8,128)S(1)} %get-tuple-element.5), channel_id=1, source_target_pairs={{0,16},{1,17},{2,18},{3,19},{4,20},{5,21},{6,22},{7,23},{8,24},{9,... | collective-permute-start | bytes 196616 | tf_op jit(solution)/shard_map/ppermute | solution.py:28
  6.0 6.1 %collective-permute-start.3 = (f32[8,2048]{1,0:T(8,128)S(1)}, f32[8,2048]{1,0:T(8,128)S(1)}, u32[]{:S(2)}, u32[]{:S(2)}) collective-permute-start(f32[8,2048]{1,0:T(8,128)S(1)} %get-tuple-element.5), channel_id=1, source_target_pairs={{0,8},{1,9},{2,10},{3,11},{4,12},{5,13},{6,14},{7,15},{8,0},{9,1},... | collective-permute-start | bytes 196616 | tf_op jit(solution)/shard_map/ppermute | solution.py:28
  6.6 5.6 %collective-permute-start = (f32[8,2048]{1,0:T(8,128)S(1)}, f32[8,2048]{1,0:T(8,128)S(1)}, u32[]{:S(2)}, u32[]{:S(2)}) collective-permute-start(f32[8,2048]{1,0:T(8,128)S(1)} %get-tuple-element.5), channel_id=1, source_target_pairs={{0,1},{1,0},{2,3},{3,2},{4,5},{5,4},{6,7},{7,6},{8,9},{9,8},{10,11... | collective-permute-start | bytes 196616 | tf_op jit(solution)/shard_map/ppermute | solution.py:28
  8.3 0.7 %copy-start.2 = (f32[1536]{0:T(1024)S(1)}, f32[1536]{0:T(1024)}, u32[]{:S(2)}) copy-start(f32[1536]{0:T(1024)} %param.11) | copy-start | bytes 18436
  9.0 0.7 %copy-start.4 = (f32[2]{0:T(128)S(1)}, f32[2]{0:T(128)}, u32[]{:S(2)}) copy-start(f32[2]{0:T(128)} %param.12) | copy-start | bytes 28
  9.6 0.7 %copy-start.3 = (f32[512]{0:T(512)S(1)}, f32[512]{0:T(512)}, u32[]{:S(2)}) copy-start(f32[512]{0:T(512)} %param.10) | copy-start | bytes 6148
  10.3 0.7 %copy-start.5 = (f32[2]{0:T(128)S(1)}, f32[2]{0:T(128)}, u32[]{:S(2)}) copy-start(f32[2]{0:T(128)} %param.13) | copy-start | bytes 28
  11.0 0.7 %copy-start.6 = (s32[1,16]{1,0:T(1,128)S(1)}, s32[1,16]{1,0:T(1,128)}, u32[]{:S(2)}) copy-start(s32[1,16]{1,0:T(1,128)} %param.15) | copy-start | bytes 196
  12.1 6.7 %collective-permute-start.4 = (f32[32,2048]{1,0:T(8,128)S(1)}, f32[32,2048]{1,0:T(8,128)S(1)}, u32[]{:S(2)}, u32[]{:S(2)}) collective-permute-start(f32[32,2048]{1,0:T(8,128)S(1)} %pad_maximum_fusion), channel_id=1, source_target_pairs={{0,2},{1,3},{2,0},{3,1},{4,6},{5,7},{6,4},{7,5},{8,10},{9,11},{10,... | collective-permute-start | bytes 786440 | tf_op jit(solution)/shard_map/ppermute | solution.py:28
  12.2 6.0 %collective-permute-start.5 = (f32[16,2048]{1,0:T(8,128)S(1)}, f32[16,2048]{1,0:T(8,128)S(1)}, u32[]{:S(2)}, u32[]{:S(2)}) collective-permute-start(f32[16,2048]{1,0:T(8,128)S(1)} %pad_maximum_fusion.1), channel_id=1, source_target_pairs={{0,4},{1,5},{2,6},{3,7},{4,0},{5,1},{6,2},{7,3},{8,12},{9,13},{10,... | collective-permute-start | bytes 393224 | tf_op jit(solution)/shard_map/ppermute | solution.py:28
  18.1 0.6 %copy-start = (f32[16,2048]{1,0:T(8,128)}, f32[16,2048]{1,0:T(8,128)S(1)}, u32[]{:S(2)}) copy-start(f32[16,2048]{1,0:T(8,128)S(1)} %collective-permute-done.5) | copy-start | bytes 393220
  18.8 0.9 %slice-start = ((f32[16,2048]{1,0:T(8,128)}), f32[16,1536]{1,0:T(8,128)S(1)}, s32[]{:S(2)}) async-start(f32[16,2048]{1,0:T(8,128)} %copy-done), calls=%async_computation | async-start | bytes 196608 | tf_op jit(solution)/shard_map/slice | solution.py:72
  19.7 0.8 %slice-start.1 = ((f32[16,2048]{1,0:T(8,128)}), f32[16,512]{1,0:T(8,128)S(1)}, s32[]{:S(2)}) async-start(f32[16,2048]{1,0:T(8,128)} %copy-done), calls=%async_computation.1 | async-start | bytes 65536 | tf_op jit(solution)/shard_map/slice | solution.py:69
  20.4 0.7 %copy-start.7 = (f32[2]{0:T(128)S(1)}, f32[2]{0:T(128)}, u32[]{:S(2)}) copy-start(f32[2]{0:T(128)} %param.14) | copy-start | bytes 28
  21.4 3.8 %collective-permute-start.6 = (f32[2,16,64]{2,1,0:T(8,128)S(1)}, f32[2,16,64]{2,1,0:T(8,128)S(1)}, u32[]{:S(2)}, u32[]{:S(2)}) collective-permute-start(f32[2,16,64]{2,1,0:T(8,128)S(1)} %copy.14), channel_id=1, source_target_pairs={{0,4},{1,5},{2,6},{3,7},{4,0},{5,1},{6,2},{7,3},{8,12},{9,13},{10,... | collective-permute-start | bytes 24584 | tf_op jit(solution)/shard_map/ppermute | solution.py:81

commit v2 on v1

v2 whole, which is shorter than its diff:
```python
import functools

import jax
import jax.numpy as jnp
from jax import lax
from jax.experimental import pallas as pl
from jax.experimental.pallas import tpu as pltpu
from jax.sharding import PartitionSpec as P


AXES = ("pts", "tau")
DIRECT = 4
VMEM = pl.BlockSpec(memory_space=pltpu.VMEM)
PARAMS = pltpu.CompilerParams(vmem_limit_bytes=8 * 1024 * 1024)
SMEM = pl.BlockSpec(memory_space=pltpu.SMEM)


def layout(mesh):
    points, groups = mesh.shape["pts"], mesh.shape["tau"]
    cores = 2 if points % 2 == 0 else 1
    pairs = 2 if points % (2 * cores) == 0 else 1
    return points // (pairs * cores), pairs, cores, groups


def strides_of(mesh):
    sizes = layout(mesh)
    return (sizes[1] * sizes[2] * sizes[3], sizes[2] * sizes[3], sizes[3], 1)


def coordinates(mesh):
    me = lax.axis_index("pts") * mesh.shape["tau"] + lax.axis_index("tau")
    return [lax.rem(lax.div(me, stride), size) for size, stride in zip(layout(mesh), strides_of(mesh))]


def direct(mesh, dim):
    size = layout(mesh)[dim]
    return size <= DIRECT and size & (size - 1) == 0


def gather(mesh, dim, block):
    sizes, stride = layout(mesh), strides_of(mesh)[dim]
    size, n = sizes[dim], sizes[0] * strides_of(mesh)[0]
    if direct(mesh, dim):
        blocks = [block]
        for step in range(size - 1, 0, -1):
            moved = [(i, i + ((((i // stride) % size) ^ step) - (i // stride) % size) * stride) for i in range(n)]
            blocks.append(lax.ppermute(block, AXES, moved))
        return blocks
    mine = coordinates(mesh)[dim]
    firsts = [i for i in range(n) if (i // stride) % size == 0]
    members = [[i + k * stride for k in range(size)] for i in firsts]
    every = lax.all_gather(block, AXES, axis=0, axis_index_groups=members)
    return [every[(mine + k) % size] for k in range(size)]


def halves(x):
    high = x.astype(jnp.bfloat16)
    return high, (x - high.astype(jnp.float32)).astype(jnp.bfloat16)


def dot(a, b):
    return lax.dot_general(a, b, (((1,), (1,)), ((), ())), preferred_element_type=jnp.float32)


def products(left, right):
    (a, a_low), (b, b_low) = halves(left), halves(right)
    return dot(a, b) + (dot(a, b_low) + dot(a_low, b))


def prepare_kernel(tau, weight, frequency, occupied_energy, virtual_energy, live, decay, mixing, mask):
    n_occupied = occupied_energy.shape[1]
    for t in range(tau.shape[0]):
        decay[t : t + 1, :n_occupied] = jnp.exp(occupied_energy[...] * tau[t])
        decay[t : t + 1, n_occupied:] = jnp.exp(-virtual_energy[...] * tau[t])
        for k in range(frequency.shape[0]):
            row = k * tau.shape[0] + t
            angle = jnp.full((1, 128), frequency[k] * tau[t], jnp.float32)
            mixing[row : row + 1, :] = -2.0 * weight[t] * jnp.cos(angle)
    width, blocks = mask.shape[1], live.shape[1]
    column = lax.broadcasted_iota(jnp.int32, (blocks, width), 1)
    block = lax.broadcasted_iota(jnp.int32, (blocks, width), 0)
    spread = jnp.where(lax.div(column, width // blocks) == block, 1.0, 0.0)
    marks = jnp.broadcast_to(live[...].astype(jnp.float32), (8, blocks))
    mask[...] = jnp.dot(marks, spread, preferred_element_type=jnp.float32)


def chi_parts(n_occupied, rows, columns, decay, mixing, n_frequencies):
    n_times = decay.shape[0]
    cols = jnp.concatenate([c[...] for c in columns], axis=0)
    green = []
    for part in (slice(None, n_occupied), slice(n_occupied, None)):
        left = jnp.concatenate([rows[:, part] * decay[t : t + 1, part] for t in range(n_times)], axis=0)
        green.append(products(left, cols[:, part]))
    n_rows = rows.shape[0]
    pair = green[0] * green[1]
    out = []
    for k in range(n_frequencies):
        total = None
        for t in range(n_times):
            row = k * n_times + t
            term = pair[t * n_rows : (t + 1) * n_rows] * mixing[row : row + 1, :1]
            total = term if total is None else total + term
        out.append(total)
    return out


def there_kernel(n_occupied, n_frequencies, rows, *refs):
    columns, (decay, mixing, out) = refs[:-3], refs[-3:]
    for k, chi in enumerate(chi_parts(n_occupied, rows, columns, decay, mixing, n_frequencies)):
        out[k] = chi


def spread_of(mesh, device_pts, pair, width, here):
    sizes = layout(mesh)
    at = coordinates(mesh)
    row = lax.broadcasted_iota(jnp.int32, (width, here), 0)
    column = lax.broadcasted_iota(jnp.int32, (width, here), 1)
    place = lax.div(column, device_pts)
    core = lax.rem(place, sizes[2])
    at_pair = lax.rem(lax.div(place, sizes[2]), sizes[1])
    far = lax.div(place, sizes[2] * sizes[1])
    if direct(mesh, 0):
        step = far ^ at[0]
        nth = (core ^ at[2]) * sizes[0] + jnp.where(step == 0, 0, sizes[0] - step)
    else:
        nth = (core ^ at[2]) * sizes[0] + lax.rem(far - at[0] + sizes[0], sizes[0])
    source = nth * device_pts + lax.rem(column, device_pts)
    return jnp.where((source == row) & (at_pair == pair), 1.0, 0.0)


def here_kernel(mesh, n_occupied, n_frequencies, device_pts, rows, *refs):
    columns, (decay, mixing, mask, out) = refs[:-4], refs[-4:]
    chi = jnp.concatenate(chi_parts(n_occupied, rows, columns, decay, mixing, n_frequencies), axis=0)
    pair = coordinates(mesh)[1]
    spread = spread_of(mesh, device_pts, pair, chi.shape[1], out.shape[1])
    out[...] = jnp.dot(chi, spread, precision=lax.Precision.HIGHEST, preferred_element_type=jnp.float32) * mask[0:1, :]


def join_kernel(mesh, device_pts, here, mask, *refs):
    back, out = refs[:-1], refs[-1]
    total = here[...]
    pair = coordinates(mesh)[1]
    for step, came in enumerate(back, 1):
        chi = came[...].reshape(-1, came.shape[2])
        spread = spread_of(mesh, device_pts, pair ^ step, chi.shape[1], out.shape[1])
        moved = jnp.dot(chi, spread, precision=lax.Precision.HIGHEST, preferred_element_type=jnp.float32)
        total = total + moved * mask[0:1, :]
    out[...] = total


def on_device(
    mesh,
    occupied_values,
    virtual_values,
    occupied_energy,
    virtual_energy,
    tau_points,
    tau_weights,
    frequencies,
    pair_live,
):
    device_pts, n_occupied = occupied_values.shape
    n_all = n_occupied + virtual_values.shape[1]
    n_times, n_frequencies = tau_points.shape[0], frequencies.shape[0]
    far, pairs, cores, groups = layout(mesh)
    n = far * pairs * cores * groups
    f32 = jnp.float32

    own = jnp.pad(occupied_values, ((0, 0), (0, n_all - n_occupied))) + jnp.pad(virtual_values, ((0, 0), (n_occupied, 0)))
    row_blocks = gather(mesh, 3, own)
    group = coordinates(mesh)[3]
    if groups == 2:
        rows = jnp.where(group == 0, jnp.concatenate(row_blocks, 0), jnp.concatenate(row_blocks[::-1], 0))
    else:
        rows = jnp.roll(jnp.concatenate(row_blocks, 0), group * device_pts, axis=0)
    far_blocks = gather(mesh, 0, own)
    row_sets = gather(mesh, 1, rows)
    column_sets = gather(mesh, 2, jnp.concatenate(far_blocks, axis=0))

    decay, mixing, mask = pl.pallas_call(
        prepare_kernel,
        name="prepare",
        out_shape=[
            jax.ShapeDtypeStruct((n_times, n_all), f32),
            jax.ShapeDtypeStruct((n_times * n_frequencies, 128), f32),
            jax.ShapeDtypeStruct((8, far * pairs * cores * device_pts), f32),
        ],
        in_specs=[SMEM] * 3 + [VMEM] * 3,
        out_specs=[VMEM] * 3,
        compiler_params=PARAMS,
    )(tau_points, tau_weights, frequencies, occupied_energy[None], virtual_energy[None], pair_live)

    n_rows, width = rows.shape[0], far * cores * device_pts
    cost = pl.CostEstimate(flops=6 * n_times * n_rows * width * n_all, bytes_accessed=4 * n_all * (width + n_rows), transcendentals=0)
    back = []
    for step in range(1, pairs):
        there = pl.pallas_call(
            functools.partial(there_kernel, n_occupied, n_frequencies),
            name="there",
            out_shape=jax.ShapeDtypeStruct((n_frequencies, n_rows, width), f32),
            in_specs=[VMEM] * (3 + len(column_sets)),
            out_specs=VMEM,
            cost_estimate=cost,
            compiler_params=PARAMS,
        )(row_sets[step], *column_sets, decay, mixing)
        swap = cores * groups * step
        back.append(lax.ppermute(there, AXES, [(i, i ^ swap) for i in range(n)]))
    here = pl.pallas_call(
        functools.partial(here_kernel, mesh, n_occupied, n_frequencies, device_pts),
        name="here",
        out_shape=jax.ShapeDtypeStruct((n_frequencies * n_rows, mask.shape[1]), f32),
        in_specs=[VMEM] * (4 + len(column_sets)),
        out_specs=VMEM,
        cost_estimate=cost,
        compiler_params=PARAMS,
    )(rows, *column_sets, decay, mixing, mask)
    out = pl.pallas_call(
        functools.partial(join_kernel, mesh, device_pts),
        name="join",
        out_shape=jax.ShapeDtypeStruct((n_frequencies * n_rows, mask.shape[1]), f32),
        in_specs=[VMEM] * (2 + len(back)),
        out_specs=VMEM,
        compiler_params=PARAMS,
    )(here, mask, *back)
    return out.reshape(n_frequencies, n_rows, 1, mask.shape[1])


def solution(mesh):
    return jax.shard_map(
        functools.partial(on_device, mesh),
        mesh=mesh,
        in_specs=(P(AXES, None), P(AXES, None), P(), P(), P(), P(), P(), P("pts", None)),
        out_specs=P(None, "pts", "tau", None),
        check_vma=False,
    )
```

time: 26.6 us -> 23.8 us (0.89)
  local copies, waits for them, and re-layouts: 6.45 us -> 0.69 us
  waiting for transfers between devices: 5.58 us -> 9.07 us
  matrix products: 2.92 us -> 0 us
  Pallas kernels: 0 us -> 2.3 us
  other arithmetic: 0.43 us -> 0.84 us
    unnamed x20 -> x12, local copies, waits for them, and re-layouts: 4.82 us -> 0.69 us
    ppermute x7, waiting for transfers between devices: 5.58 us -> 9.07 us  [the longest x6 7.31 us: gather(): blocks.append(lax.ppermute(block, AXES, moved))]
    dot_general x8 -> x0, matrix products: 2.92 us -> none  [the longest x2 0.88 us: chi_of(): jnp.einsum('trw,nw->trn', part[None, :, n_occupied:] * virtual_decay, col...]
    pallas_call x0 -> x4, Pallas kernels: none -> 2.3 us  [the longest x1 0.78 us: on_device(): pl.pallas_call(functools.partial(join_kernel, mesh, device_pts), name='jo...]
    slice x4 -> x0, local copies, waits for them, and re-layouts: 1.18 us -> none  [the longest x2 0.87 us: chi_of(): part[None, :, n_occupied:] * virtual_decay]
    add x2 -> x1, other arithmetic: 0.14 us -> 0.81 us  [on_device(): jnp.pad(occupied_values, ((0, 0), (0, n_all - n_occupied)))]
  transfers between devices with their start and end apart: 7 -> 7, of which waited for: 2 -> 4; matrix products, arithmetic and copies ran while one was open for 7% -> 0% of each run, Pallas kernels for 0% -> 5%
where the time goes in v2:
time: 23.8 us; the launch traced here: 23.6 us
  starting transfers between devices  10.6 us (45%)
  waiting for transfers between devices  9.07 us (38%)
  Pallas kernels  2.3 us (10%)
  other arithmetic  0.84 us (4%)
  local copies, waits for them, and re-layouts  0.69 us (3%)
    ppermute x6, starting transfers between devices, gather(): blocks.append(lax.ppermute(block, AXES, moved))  9.01 us
    ppermute x6, waiting for transfers between devices, gather(): blocks.append(lax.ppermute(block, AXES, moved))  7.31 us
    ppermute x1, waiting for transfers between devices, on_device(): back.append(lax.ppermute(there, AXES, [(i, i ^ swap) for i in range(n)]))  1.76 us
    ppermute x1, starting transfers between devices, on_device(): back.append(lax.ppermute(there, AXES, [(i, i ^ swap) for i in range(n)]))  1.56 us
    add x1, other arithmetic, on_device(): jnp.pad(occupied_values, ((0, 0), (0, n_all - n_occupied)))  0.81 us
    pallas_call x1, Pallas kernels, on_device(): pl.pallas_call(functools.partial(join_kernel, mesh, device_pts), name='jo...  0.78 us
    pallas_call x1, Pallas kernels, on_device(): pl.pallas_call(prepare_kernel, name='prepare', out_shape=[jax.ShapeDtypeS...  0.7 us
    unnamed x12, local copies, waits for them, and re-layouts  0.69 us
  transfers between devices with their start and end apart: 7, of which 4 were waited for; matrix products, arithmetic and copies ran while one was open for 0% of the time, Pallas kernels for 5%

profile of v2, /device:TPU:0, one launch (start us, length us, event | category | flops | bytes accessed | tf_op | source)
XLA Modules:
  0.0 23.6 jit_solution(5929534416613757900)
XLA Ops:
  0.0 0.8 %pad_add_fusion = f32[8,2048]{1,0:T(8,128)S(1)} fusion(f32[8,1536]{1,0:T(8,128)} %param.9, f32[8,512]{1,0:T(8,128)} %param.8), kind=kLoop, calls=%fused_computation.2 | loop fusion | flops 16384 | bytes 131072 | tf_op jit(solution)/shard_map/add | solution.py:169
  0.8 3.1 %collective-permute-start.3 = (f32[8,2048]{1,0:T(8,128)S(1)}, f32[8,2048]{1,0:T(8,128)S(1)}, u32[]{:S(2)}, u32[]{:S(2)}) collective-permute-start(f32[8,2048]{1,0:T(8,128)S(1)} %pad_add_fusion), channel_id=1, source_target_pairs={{0,8},{1,9},{2,10},{3,11},{4,12},{5,13},{6,14},{7,15},{8,0},{9,1},... | collective-permute-start | bytes 196616 | tf_op jit(solution)/shard_map/ppermute | solution.py:47
  3.9 2.6 %collective-permute-start.2 = (f32[8,2048]{1,0:T(8,128)S(1)}, f32[8,2048]{1,0:T(8,128)S(1)}, u32[]{:S(2)}, u32[]{:S(2)}) collective-permute-start(f32[8,2048]{1,0:T(8,128)S(1)} %pad_add_fusion), channel_id=1, source_target_pairs={{0,16},{1,17},{2,18},{3,19},{4,20},{5,21},{6,22},{7,23},{8,24},{9,... | collective-permute-start | bytes 196616 | tf_op jit(solution)/shard_map/ppermute | solution.py:47
  6.4 0.0 collective-permute-start.1
  6.5 1.7 %collective-permute-start = (f32[8,2048]{1,0:T(8,128)S(1)}, f32[8,2048]{1,0:T(8,128)S(1)}, u32[]{:S(2)}, u32[]{:S(2)}) collective-permute-start(f32[8,2048]{1,0:T(8,128)S(1)} %pad_add_fusion), channel_id=1, source_target_pairs={{0,1},{1,0},{2,3},{3,2},{4,5},{5,4},{6,7},{7,6},{8,9},{9,8},{10,11... | collective-permute-start | bytes 196616 | tf_op jit(solution)/shard_map/ppermute | solution.py:47
  8.2 0.0 collective-permute-done.3
  8.2 2.9 %collective-permute-done.2 = f32[8,2048]{1,0:T(8,128)S(1)} collective-permute-done((f32[8,2048]{1,0:T(8,128)S(1)}, f32[8,2048]{1,0:T(8,128)S(1)}, u32[]{:S(2)}, u32[]{:S(2)}) %collective-permute-start.2) | collective-permute-done | bytes 65568 | tf_op jit(solution)/shard_map/ppermute | solution.py:47
  11.1 1.4 %collective-permute-done.1 = f32[8,2048]{1,0:T(8,128)S(1)} collective-permute-done((f32[8,2048]{1,0:T(8,128)S(1)}, f32[8,2048]{1,0:T(8,128)S(1)}, u32[]{:S(2)}, u32[]{:S(2)}) %collective-permute-start.1) | collective-permute-done | bytes 65568 | tf_op jit(solution)/shard_map/ppermute | solution.py:47
  12.5 0.0 copy-start.5
  12.6 0.1 collective-permute-start.4
  12.7 1.6 %collective-permute-start.5 = (f32[16,2048]{1,0:T(8,128)S(1)}, f32[16,2048]{1,0:T(8,128)S(1)}, u32[]{:S(2)}, u32[]{:S(2)}) collective-permute-start(f32[16,2048]{1,0:T(8,128)S(1)} %maximum_select_fusion.rows), channel_id=1, source_target_pairs={{0,4},{1,5},{2,6},{3,7},{4,0},{5,1},{6,2},{7,3},{8,12},{9,13},{10,... | collective-permute-start | bytes 393224 | tf_op jit(solution)/shard_map/ppermute | solution.py:47
  14.2 0.0 copy-start.1
  14.3 0.0 copy-start.2
  14.3 0.0 copy-start.3
  14.3 0.6 %copy-done = f32[512]{0:T(512)S(1)} copy-done((f32[512]{0:T(512)S(1)}, f32[512]{0:T(512)}, u32[]{:S(2)}) %copy-start) | copy-done | bytes 2072
  14.9 0.0 copy-done.2
  14.9 0.0 copy-done.3
  14.9 0.7 %prepare.1 = (f32[2,2048]{1,0:T(2,128)S(1)}, f32[4,128]{1,0:T(4,128)S(1)}, f32[8,128]{1,0:T(8,128)S(1)}) custom-call(f32[2]{0:T(128)S(1)} %copy-done.1, f32[2]{0:T(128)S(1)} %copy-done.2, f32[2]{0:T(128)S(1)} %copy-done.3, f32[1,512]{1,0:T(1,128)S(1)} %bitcast.4, f32[1,1536]{1,0:T(1,128)S(1)} %broadcast_in_dim.7.virtual_energy, s32[1,16]{1,0:T(1,128)S(1)} %copy-done.4), custom_call_target="tpu_custom_call" | custom-call | tf_op jit(solution)/shard_map/prepare/pallas_call | solution.py:180
  15.6 3.0 %collective-permute-done.5.rows = f32[16,2048]{1,0:T(8,128)S(1)} collective-permute-done((f32[16,2048]{1,0:T(8,128)S(1)}, f32[16,2048]{1,0:T(8,128)S(1)}, u32[]{:S(2)}, u32[]{:S(2)}) %collective-permute-start.5) | collective-permute-done | bytes 131104 | tf_op jit(solution)/shard_map/ppermute | solution.py:47
  18.6 0.3 %there.1 = f32[2,16,64]{2,1,0:T(8,128)S(1)} custom-call(f32[16,2048]{1,0:T(8,128)S(1)} %collective-permute-done.5.rows, f32[32,2048]{1,0:T(8,128)S(1)} %pad_maximum_fusion.refs_0_, f32[32,2048]{1,0:T(8,128)S(1)} %collective-permute-done.4.refs_1_, f32[2,2048]{1,0:T(2,128)S(1)} %get-tuple-element.8.refs_2_, f32[4,128]{1,0:T(4,128)S(1)} %get-tuple-element.9.refs_3_), custom_call_target="tpu_custom_call" | custom-call | flops 25165824 | bytes 655360 | tf_op jit(solution)/shard_map/there/pallas_call | solution.py:197
  19.0 1.6 %collective-permute-start.6 = (f32[2,16,64]{2,1,0:T(8,128)S(1)}, f32[2,16,64]{2,1,0:T(8,128)S(1)}, u32[]{:S(2)}, u32[]{:S(2)}) collective-permute-start(f32[2,16,64]{2,1,0:T(8,128)S(1)} %there.1), channel_id=1, source_target_pairs={{0,4},{1,5},{2,6},{3,7},{4,0},{5,1},{6,2},{7,3},{8,12},{9,13},{10,... | collective-permute-start | bytes 24584 | tf_op jit(solution)/shard_map/ppermute | solution.py:207
  20.5 0.5 %here.1 = f32[32,128]{1,0:T(8,128)S(1)} custom-call(f32[16,2048]{1,0:T(8,128)S(1)} %maximum_select_fusion.rows, f32[32,2048]{1,0:T(8,128)S(1)} %pad_maximum_fusion.refs_0_, f32[32,2048]{1,0:T(8,128)S(1)} %collective-permute-done.4.refs_1_, f32[2,2048]{1,0:T(2,128)S(1)} %get-tuple-element.8.refs_2_, f32[4,128]{1,0:T(4,128)S(1)} %get-tuple-element.9.refs_3_, ...), custom_call_target="tpu_custom_call" | custom-call | flops 25165824 | bytes 655360 | tf_op jit(solution)/shard_map/here/pallas_call | solution.py:208
  21.0 1.8 %collective-permute-done.6.refs_0_ = f32[2,16,64]{2,1,0:T(8,128)S(1)} collective-permute-done((f32[2,16,64]{2,1,0:T(8,128)S(1)}, f32[2,16,64]{2,1,0:T(8,128)S(1)}, u32[]{:S(2)}, u32[]{:S(2)}) %collective-permute-start.6) | collective-permute-done | bytes 8224 | tf_op jit(solution)/shard_map/ppermute | solution.py:207
  22.8 0.8 %join.1 = f32[32,128]{1,0:T(8,128)} custom-call(f32[32,128]{1,0:T(8,128)S(1)} %here.1, f32[8,128]{1,0:T(8,128)S(1)} %get-tuple-element.10.refs_4_.mask, f32[2,16,64]{2,1,0:T(8,128)S(1)} %collective-permute-done.6.refs_0_), custom_call_target="tpu_custom_call" | custom-call | tf_op jit(solution)/shard_map/join/pallas_call | solution.py:217
  (10 shorter events, 0.1 us)
Async XLA Ops:
  0.8 7.4 %collective-permute-start.3 = (f32[8,2048]{1,0:T(8,128)S(1)}, f32[8,2048]{1,0:T(8,128)S(1)}, u32[]{:S(2)}, u32[]{:S(2)}) collective-permute-start(f32[8,2048]{1,0:T(8,128)S(1)} %pad_add_fusion), channel_id=1, source_target_pairs={{0,8},{1,9},{2,10},{3,11},{4,12},{5,13},{6,14},{7,15},{8,0},{9,1},... | collective-permute-start | bytes 196616 | tf_op jit(solution)/shard_map/ppermute | solution.py:47
  3.9 7.3 %collective-permute-start.2 = (f32[8,2048]{1,0:T(8,128)S(1)}, f32[8,2048]{1,0:T(8,128)S(1)}, u32[]{:S(2)}, u32[]{:S(2)}) collective-permute-start(f32[8,2048]{1,0:T(8,128)S(1)} %pad_add_fusion), channel_id=1, source_target_pairs={{0,16},{1,17},{2,18},{3,19},{4,20},{5,21},{6,22},{7,23},{8,24},{9,... | collective-permute-start | bytes 196616 | tf_op jit(solution)/shard_map/ppermute | solution.py:47
  6.4 6.1 %collective-permute-start.1 = (f32[8,2048]{1,0:T(8,128)S(1)}, f32[8,2048]{1,0:T(8,128)S(1)}, u32[]{:S(2)}, u32[]{:S(2)}) collective-permute-start(f32[8,2048]{1,0:T(8,128)S(1)} %pad_add_fusion), channel_id=1, source_target_pairs={{0,24},{1,25},{2,26},{3,27},{4,28},{5,29},{6,30},{7,31},{8,16},{9,... | collective-permute-start | bytes 196616 | tf_op jit(solution)/shard_map/ppermute | solution.py:47
  6.5 6.2 %collective-permute-start = (f32[8,2048]{1,0:T(8,128)S(1)}, f32[8,2048]{1,0:T(8,128)S(1)}, u32[]{:S(2)}, u32[]{:S(2)}) collective-permute-start(f32[8,2048]{1,0:T(8,128)S(1)} %pad_add_fusion), channel_id=1, source_target_pairs={{0,1},{1,0},{2,3},{3,2},{4,5},{5,4},{6,7},{7,6},{8,9},{9,8},{10,11... | collective-permute-start | bytes 196616 | tf_op jit(solution)/shard_map/ppermute | solution.py:47
  12.5 1.7 %copy-start.5 = (f32[1536]{0:T(1024)S(1)}, f32[1536]{0:T(1024)}, u32[]{:S(2)}) copy-start(f32[1536]{0:T(1024)} %param.11) | copy-start | bytes 18436
  12.6 6.1 %collective-permute-start.4 = (f32[32,2048]{1,0:T(8,128)S(1)}, f32[32,2048]{1,0:T(8,128)S(1)}, u32[]{:S(2)}, u32[]{:S(2)}) collective-permute-start(f32[32,2048]{1,0:T(8,128)S(1)} %pad_maximum_fusion.refs_0_), channel_id=1, source_target_pairs={{0,2},{1,3},{2,0},{3,1},{4,6},{5,7},{6,4},{7,5},{8,10},{9,11},{10,... | collective-permute-start | bytes 786440 | tf_op jit(solution)/shard_map/ppermute | solution.py:47
  12.7 6.0 %collective-permute-start.5 = (f32[16,2048]{1,0:T(8,128)S(1)}, f32[16,2048]{1,0:T(8,128)S(1)}, u32[]{:S(2)}, u32[]{:S(2)}) collective-permute-start(f32[16,2048]{1,0:T(8,128)S(1)} %maximum_select_fusion.rows), channel_id=1, source_target_pairs={{0,4},{1,5},{2,6},{3,7},{4,0},{5,1},{6,2},{7,3},{8,12},{9,13},{10,... | collective-permute-start | bytes 393224 | tf_op jit(solution)/shard_map/ppermute | solution.py:47
  14.2 0.7 %copy-start = (f32[512]{0:T(512)S(1)}, f32[512]{0:T(512)}, u32[]{:S(2)}) copy-start(f32[512]{0:T(512)} %param.10) | copy-start | bytes 6148
  14.2 0.7 %copy-start.4 = (s32[1,16]{1,0:T(1,128)S(1)}, s32[1,16]{1,0:T(1,128)}, u32[]{:S(2)}) copy-start(s32[1,16]{1,0:T(1,128)} %live.1) | copy-start | bytes 196
  14.2 0.7 %copy-start.1 = (f32[2]{0:T(128)S(1)}, f32[2]{0:T(128)}, u32[]{:S(2)}) copy-start(f32[2]{0:T(128)} %tau.1) | copy-start | bytes 28
  14.3 0.7 %copy-start.2 = (f32[2]{0:T(128)S(1)}, f32[2]{0:T(128)}, u32[]{:S(2)}) copy-start(f32[2]{0:T(128)} %weight.1) | copy-start | bytes 28
  14.3 0.7 %copy-start.3 = (f32[2]{0:T(128)S(1)}, f32[2]{0:T(128)}, u32[]{:S(2)}) copy-start(f32[2]{0:T(128)} %frequency.1) | copy-start | bytes 28
  19.0 3.8 %collective-permute-start.6 = (f32[2,16,64]{2,1,0:T(8,128)S(1)}, f32[2,16,64]{2,1,0:T(8,128)S(1)}, u32[]{:S(2)}, u32[]{:S(2)}) collective-permute-start(f32[2,16,64]{2,1,0:T(8,128)S(1)} %there.1), channel_id=1, source_target_pairs={{0,4},{1,5},{2,6},{3,7},{4,0},{5,1},{6,2},{7,3},{8,12},{9,13},{10,... | collective-permute-start | bytes 24584 | tf_op jit(solution)/shard_map/ppermute | solution.py:207

commit v3 on v2

--- a/solution.py
+++ b/solution.py
@@ -37,14 +37,29 @@
     return size <= DIRECT and size & (size - 1) == 0
 
 
+def crossing(mesh, dim, step):
+    return (dim, step) in CROSSING and layout(mesh)[2] == 2 and direct(mesh, dim)
+
+
+def moves(mesh, dim, step):
+    sizes, stride = layout(mesh), strides_of(mesh)[dim]
+    pairs = []
+    for i in range(sizes[0] * strides_of(mesh)[0]):
+        at = (i // stride) % sizes[dim]
+        to = i + ((at ^ step) - at) * stride
+        if crossing(mesh, dim, step):
+            to += (1 - 2 * ((to // sizes[3]) % 2)) * sizes[3]
+        pairs.append((i, to))
+    return pairs
+
+
 def gather(mesh, dim, block):
     sizes, stride = layout(mesh), strides_of(mesh)[dim]
     size, n = sizes[dim], sizes[0] * strides_of(mesh)[0]
     if direct(mesh, dim):
         blocks = [block]
         for step in range(size - 1, 0, -1):
-            moved = [(i, i + ((((i // stride) % size) ^ step) - (i // stride) % size) * stride) for i in range(n)]
-            blocks.append(lax.ppermute(block, AXES, moved))
+            blocks.append(lax.ppermute(block, AXES, moves(mesh, dim, step)))
         return blocks
     mine = coordinates(mesh)[dim]
     firsts = [i for i in range(n) if (i // stride) % size == 0]
@@ -110,39 +125,42 @@
         out[k] = chi
 
 
-def spread_of(mesh, device_pts, pair, width, here):
+def spread_of(mesh, device_pts, pair, core, width, here):
     sizes = layout(mesh)
-    at = coordinates(mesh)
+    far_mine = coordinates(mesh)[0]
     row = lax.broadcasted_iota(jnp.int32, (width, here), 0)
     column = lax.broadcasted_iota(jnp.int32, (width, here), 1)
     place = lax.div(column, device_pts)
-    core = lax.rem(place, sizes[2])
+    other = lax.rem(place, sizes[2]) ^ core
     at_pair = lax.rem(lax.div(place, sizes[2]), sizes[1])
     far = lax.div(place, sizes[2] * sizes[1])
     if direct(mesh, 0):
-        step = far ^ at[0]
-        nth = (core ^ at[2]) * sizes[0] + jnp.where(step == 0, 0, sizes[0] - step)
+        step = far ^ far_mine
+        nth = jnp.where(step == 0, 0, sizes[0] - step)
+        for k in range(1, sizes[0]):
+            if crossing(mesh, 0, k):
+                other = jnp.where(step == k, 1 - other, other)
     else:
-        nth = (core ^ at[2]) * sizes[0] + lax.rem(far - at[0] + sizes[0], sizes[0])
-    source = nth * device_pts + lax.rem(column, device_pts)
+        nth = lax.rem(far - far_mine + sizes[0], sizes[0])
+    source = (other * sizes[0] + nth) * device_pts + lax.rem(column, device_pts)
     return jnp.where((source == row) & (at_pair == pair), 1.0, 0.0)
 
 
 def here_kernel(mesh, n_occupied, n_frequencies, device_pts, rows, *refs):
     columns, (decay, mixing, mask, out) = refs[:-4], refs[-4:]
     chi = jnp.concatenate(chi_parts(n_occupied, rows, columns, decay, mixing, n_frequencies), axis=0)
-    pair = coordinates(mesh)[1]
-    spread = spread_of(mesh, device_pts, pair, chi.shape[1], out.shape[1])
+    _, pair, core, _ = coordinates(mesh)
+    spread = spread_of(mesh, device_pts, pair, core, chi.shape[1], out.shape[1])
     out[...] = jnp.dot(chi, spread, precision=lax.Precision.HIGHEST, preferred_element_type=jnp.float32) * mask[0:1, :]
 
 
 def join_kernel(mesh, device_pts, here, mask, *refs):
     back, out = refs[:-1], refs[-1]
     total = here[...]
-    pair = coordinates(mesh)[1]
+    _, pair, core, _ = coordinates(mesh)
     for step, came in enumerate(back, 1):
         chi = came[...].reshape(-1, came.shape[2])
-        spread = spread_of(mesh, device_pts, pair ^ step, chi.shape[1], out.shape[1])
+        spread = spread_of(mesh, device_pts, pair ^ step, 1 - core if crossing(mesh, 1, step) else core, chi.shape[1], out.shape[1])
         moved = jnp.dot(chi, spread, precision=lax.Precision.HIGHEST, preferred_element_type=jnp.float32)
         total = total + moved * mask[0:1, :]
     out[...] = total
@@ -163,7 +181,6 @@
     n_all = n_occupied + virtual_values.shape[1]
     n_times, n_frequencies = tau_points.shape[0], frequencies.shape[0]
     far, pairs, cores, groups = layout(mesh)
-    n = far * pairs * cores * groups
     f32 = jnp.float32
 
     own = jnp.pad(occupied_values, ((0, 0), (0, n_all - n_occupied))) + jnp.pad(virtual_values, ((0, 0), (n_occupied, 0)))
@@ -175,7 +192,10 @@
         rows = jnp.roll(jnp.concatenate(row_blocks, 0), group * device_pts, axis=0)
     far_blocks = gather(mesh, 0, own)
     row_sets = gather(mesh, 1, rows)
-    column_sets = gather(mesh, 2, jnp.concatenate(far_blocks, axis=0))
+    pieces = [jnp.concatenate(far_blocks, axis=0)]
+    column_sets = []
+    for piece in pieces:
+        column_sets += gather(mesh, 2, piece)
 
     decay, mixing, mask = pl.pallas_call(
         prepare_kernel,
@@ -203,8 +223,7 @@
             cost_estimate=cost,
             compiler_params=PARAMS,
         )(row_sets[step], *column_sets, decay, mixing)
-        swap = cores * groups * step
-        back.append(lax.ppermute(there, AXES, [(i, i ^ swap) for i in range(n)]))
+        back.append(lax.ppermute(there, AXES, moves(mesh, 1, step)))
     here = pl.pallas_call(
         functools.partial(here_kernel, mesh, n_occupied, n_frequencies, device_pts),
         name="here",
@@ -225,6 +244,9 @@
     return out.reshape(n_frequencies, n_rows, 1, mask.shape[1])
 
 
+CROSSING = ((0, 1), (1, 1))
+
+
 def solution(mesh):
     return jax.shard_map(
         functools.partial(on_device, mesh),

time: 23.8 us -> 22.1 us (0.929)
  waiting for transfers between devices: 9.07 us -> 7.6 us
    ppermute x7, waiting for transfers between devices: 9.07 us -> 7.6 us  [the longest x6 6.51 us: gather(): blocks.append(lax.ppermute(block, AXES, moves(mesh, dim, step)))]
where the time goes in v3:
time: 22.1 us; the launch traced here: 21.9 us
  starting transfers between devices  10.4 us (47%)
  waiting for transfers between devices  7.6 us (34%)
  Pallas kernels  2.3 us (10%)
  other arithmetic  0.84 us (4%)
  local copies, waits for them, and re-layouts  0.69 us (3%)
    ppermute x6, starting transfers between devices, gather(): blocks.append(lax.ppermute(block, AXES, moves(mesh, dim, step)))  8.72 us
    ppermute x6, waiting for transfers between devices, gather(): blocks.append(lax.ppermute(block, AXES, moves(mesh, dim, step)))  6.51 us
    ppermute x1, starting transfers between devices, on_device(): back.append(lax.ppermute(there, AXES, moves(mesh, 1, step)))  1.65 us
    ppermute x1, waiting for transfers between devices, on_device(): back.append(lax.ppermute(there, AXES, moves(mesh, 1, step)))  1.1 us
    add x1, other arithmetic, on_device(): jnp.pad(occupied_values, ((0, 0), (0, n_all - n_occupied)))  0.81 us
    pallas_call x1, Pallas kernels, on_device(): pl.pallas_call(functools.partial(join_kernel, mesh, device_pts), name='jo...  0.78 us
    pallas_call x1, Pallas kernels, on_device(): pl.pallas_call(prepare_kernel, name='prepare', out_shape=[jax.ShapeDtypeS...  0.7 us
    unnamed x12, local copies, waits for them, and re-layouts  0.69 us
  transfers between devices with their start and end apart: 7, of which 4 were waited for; matrix products, arithmetic and copies ran while one was open for 0% of the time, Pallas kernels for 5%

profile of v3, /device:TPU:0, one launch (start us, length us, event | category | flops | bytes accessed | tf_op | source)
XLA Modules:
  0.0 21.9 jit_solution(3897971511246292647)
XLA Ops:
  0.0 0.8 %pad_add_fusion = f32[8,2048]{1,0:T(8,128)S(1)} fusion(f32[8,1536]{1,0:T(8,128)} %param.9, f32[8,512]{1,0:T(8,128)} %param.8), kind=kLoop, calls=%fused_computation.2 | loop fusion | flops 16384 | bytes 131072 | tf_op jit(solution)/shard_map/add | solution.py:186
  0.8 2.5 %collective-permute-start.3 = (f32[8,2048]{1,0:T(8,128)S(1)}, f32[8,2048]{1,0:T(8,128)S(1)}, u32[]{:S(2)}, u32[]{:S(2)}) collective-permute-start(f32[8,2048]{1,0:T(8,128)S(1)} %pad_add_fusion), channel_id=1, source_target_pairs={{0,10},{1,11},{2,8},{3,9},{4,14},{5,15},{6,12},{7,13},{8,2},{9,3},... | collective-permute-start | bytes 196616 | tf_op jit(solution)/shard_map/ppermute | solution.py:62
  3.3 2.6 %collective-permute-start.2 = (f32[8,2048]{1,0:T(8,128)S(1)}, f32[8,2048]{1,0:T(8,128)S(1)}, u32[]{:S(2)}, u32[]{:S(2)}) collective-permute-start(f32[8,2048]{1,0:T(8,128)S(1)} %pad_add_fusion), channel_id=1, source_target_pairs={{0,16},{1,17},{2,18},{3,19},{4,20},{5,21},{6,22},{7,23},{8,24},{9,... | collective-permute-start | bytes 196616 | tf_op jit(solution)/shard_map/ppermute | solution.py:62
  5.9 0.4 %collective-permute-start.1 = (f32[8,2048]{1,0:T(8,128)S(1)}, f32[8,2048]{1,0:T(8,128)S(1)}, u32[]{:S(2)}, u32[]{:S(2)}) collective-permute-start(f32[8,2048]{1,0:T(8,128)S(1)} %pad_add_fusion), channel_id=1, source_target_pairs={{0,24},{1,25},{2,26},{3,27},{4,28},{5,29},{6,30},{7,31},{8,16},{9,... | collective-permute-start | bytes 196616 | tf_op jit(solution)/shard_map/ppermute | solution.py:62
  6.3 1.5 %collective-permute-start = (f32[8,2048]{1,0:T(8,128)S(1)}, f32[8,2048]{1,0:T(8,128)S(1)}, u32[]{:S(2)}, u32[]{:S(2)}) collective-permute-start(f32[8,2048]{1,0:T(8,128)S(1)} %pad_add_fusion), channel_id=1, source_target_pairs={{0,1},{1,0},{2,3},{3,2},{4,5},{5,4},{6,7},{7,6},{8,9},{9,8},{10,11... | collective-permute-start | bytes 196616 | tf_op jit(solution)/shard_map/ppermute | solution.py:62
  7.8 0.0 collective-permute-done.3
  7.8 2.7 %collective-permute-done.2 = f32[8,2048]{1,0:T(8,128)S(1)} collective-permute-done((f32[8,2048]{1,0:T(8,128)S(1)}, f32[8,2048]{1,0:T(8,128)S(1)}, u32[]{:S(2)}, u32[]{:S(2)}) %collective-permute-start.2) | collective-permute-done | bytes 65568 | tf_op jit(solution)/shard_map/ppermute | solution.py:62
  10.5 1.7 %collective-permute-done.1 = f32[8,2048]{1,0:T(8,128)S(1)} collective-permute-done((f32[8,2048]{1,0:T(8,128)S(1)}, f32[8,2048]{1,0:T(8,128)S(1)}, u32[]{:S(2)}, u32[]{:S(2)}) %collective-permute-start.1) | collective-permute-done | bytes 65568 | tf_op jit(solution)/shard_map/ppermute | solution.py:62
  12.2 0.0 copy-start.5
  12.2 0.1 collective-permute-start.4
  12.3 1.6 %collective-permute-start.5 = (f32[16,2048]{1,0:T(8,128)S(1)}, f32[16,2048]{1,0:T(8,128)S(1)}, u32[]{:S(2)}, u32[]{:S(2)}) collective-permute-start(f32[16,2048]{1,0:T(8,128)S(1)} %maximum_select_fusion.rows), channel_id=1, source_target_pairs={{0,6},{1,7},{2,4},{3,5},{4,2},{5,3},{6,0},{7,1},{8,14},{9,15},{10,... | collective-permute-start | bytes 393224 | tf_op jit(solution)/shard_map/ppermute | solution.py:62
  14.0 0.0 copy-start.1
  14.0 0.0 copy-start.2
  14.0 0.0 copy-start.3
  14.0 0.6 %copy-done = f32[512]{0:T(512)S(1)} copy-done((f32[512]{0:T(512)S(1)}, f32[512]{0:T(512)}, u32[]{:S(2)}) %copy-start) | copy-done | bytes 2072
  14.7 0.0 copy-done.2
  14.7 0.0 copy-done.3
  14.7 0.7 %prepare.1 = (f32[2,2048]{1,0:T(2,128)S(1)}, f32[4,128]{1,0:T(4,128)S(1)}, f32[8,128]{1,0:T(8,128)S(1)}) custom-call(f32[2]{0:T(128)S(1)} %copy-done.1, f32[2]{0:T(128)S(1)} %copy-done.2, f32[2]{0:T(128)S(1)} %copy-done.3, f32[1,512]{1,0:T(1,128)S(1)} %bitcast.4, f32[1,1536]{1,0:T(1,128)S(1)} %broadcast_in_dim.7.virtual_energy, s32[1,16]{1,0:T(1,128)S(1)} %copy-done.4), custom_call_target="tpu_custom_call" | custom-call | tf_op jit(solution)/shard_map/prepare/pallas_call | solution.py:200
  15.4 2.1 %collective-permute-done.5.rows = f32[16,2048]{1,0:T(8,128)S(1)} collective-permute-done((f32[16,2048]{1,0:T(8,128)S(1)}, f32[16,2048]{1,0:T(8,128)S(1)}, u32[]{:S(2)}, u32[]{:S(2)}) %collective-permute-start.5) | collective-permute-done | bytes 131104 | tf_op jit(solution)/shard_map/ppermute | solution.py:62
  17.5 0.3 %there.1 = f32[2,16,64]{2,1,0:T(8,128)S(1)} custom-call(f32[16,2048]{1,0:T(8,128)S(1)} %collective-permute-done.5.rows, f32[32,2048]{1,0:T(8,128)S(1)} %pad_maximum_fusion.refs_0_, f32[32,2048]{1,0:T(8,128)S(1)} %collective-permute-done.4.refs_1_, f32[2,2048]{1,0:T(2,128)S(1)} %get-tuple-element.8.refs_2_, f32[4,128]{1,0:T(4,128)S(1)} %get-tuple-element.9.refs_3_), custom_call_target="tpu_custom_call" | custom-call | flops 25165824 | bytes 655360 | tf_op jit(solution)/shard_map/there/pallas_call | solution.py:217
  17.9 1.6 %collective-permute-start.6 = (f32[2,16,64]{2,1,0:T(8,128)S(1)}, f32[2,16,64]{2,1,0:T(8,128)S(1)}, u32[]{:S(2)}, u32[]{:S(2)}) collective-permute-start(f32[2,16,64]{2,1,0:T(8,128)S(1)} %there.1), channel_id=1, source_target_pairs={{0,6},{1,7},{2,4},{3,5},{4,2},{5,3},{6,0},{7,1},{8,14},{9,15},{10,... | collective-permute-start | bytes 24584 | tf_op jit(solution)/shard_map/ppermute | solution.py:226
  19.5 0.5 %here.1 = f32[32,128]{1,0:T(8,128)S(1)} custom-call(f32[16,2048]{1,0:T(8,128)S(1)} %maximum_select_fusion.rows, f32[32,2048]{1,0:T(8,128)S(1)} %pad_maximum_fusion.refs_0_, f32[32,2048]{1,0:T(8,128)S(1)} %collective-permute-done.4.refs_1_, f32[2,2048]{1,0:T(2,128)S(1)} %get-tuple-element.8.refs_2_, f32[4,128]{1,0:T(4,128)S(1)} %get-tuple-element.9.refs_3_, ...), custom_call_target="tpu_custom_call" | custom-call | flops 25165824 | bytes 655360 | tf_op jit(solution)/shard_map/here/pallas_call | solution.py:227
  20.0 1.1 %collective-permute-done.6.refs_0_ = f32[2,16,64]{2,1,0:T(8,128)S(1)} collective-permute-done((f32[2,16,64]{2,1,0:T(8,128)S(1)}, f32[2,16,64]{2,1,0:T(8,128)S(1)}, u32[]{:S(2)}, u32[]{:S(2)}) %collective-permute-start.6) | collective-permute-done | bytes 8224 | tf_op jit(solution)/shard_map/ppermute | solution.py:226
  21.1 0.8 %join.1 = f32[32,128]{1,0:T(8,128)} custom-call(f32[32,128]{1,0:T(8,128)S(1)} %here.1, f32[8,128]{1,0:T(8,128)S(1)} %get-tuple-element.10.refs_4_.mask, f32[2,16,64]{2,1,0:T(8,128)S(1)} %collective-permute-done.6.refs_0_), custom_call_target="tpu_custom_call" | custom-call | tf_op jit(solution)/shard_map/join/pallas_call | solution.py:236
  (10 shorter events, 0.1 us)
Async XLA Ops:
  0.8 7.0 %collective-permute-start.3 = (f32[8,2048]{1,0:T(8,128)S(1)}, f32[8,2048]{1,0:T(8,128)S(1)}, u32[]{:S(2)}, u32[]{:S(2)}) collective-permute-start(f32[8,2048]{1,0:T(8,128)S(1)} %pad_add_fusion), channel_id=1, source_target_pairs={{0,10},{1,11},{2,8},{3,9},{4,14},{5,15},{6,12},{7,13},{8,2},{9,3},... | collective-permute-start | bytes 196616 | tf_op jit(solution)/shard_map/ppermute | solution.py:62
  3.3 7.2 %collective-permute-start.2 = (f32[8,2048]{1,0:T(8,128)S(1)}, f32[8,2048]{1,0:T(8,128)S(1)}, u32[]{:S(2)}, u32[]{:S(2)}) collective-permute-start(f32[8,2048]{1,0:T(8,128)S(1)} %pad_add_fusion), channel_id=1, source_target_pairs={{0,16},{1,17},{2,18},{3,19},{4,20},{5,21},{6,22},{7,23},{8,24},{9,... | collective-permute-start | bytes 196616 | tf_op jit(solution)/shard_map/ppermute | solution.py:62
  5.9 6.3 %collective-permute-start.1 = (f32[8,2048]{1,0:T(8,128)S(1)}, f32[8,2048]{1,0:T(8,128)S(1)}, u32[]{:S(2)}, u32[]{:S(2)}) collective-permute-start(f32[8,2048]{1,0:T(8,128)S(1)} %pad_add_fusion), channel_id=1, source_target_pairs={{0,24},{1,25},{2,26},{3,27},{4,28},{5,29},{6,30},{7,31},{8,16},{9,... | collective-permute-start | bytes 196616 | tf_op jit(solution)/shard_map/ppermute | solution.py:62
  6.3 6.0 %collective-permute-start = (f32[8,2048]{1,0:T(8,128)S(1)}, f32[8,2048]{1,0:T(8,128)S(1)}, u32[]{:S(2)}, u32[]{:S(2)}) collective-permute-start(f32[8,2048]{1,0:T(8,128)S(1)} %pad_add_fusion), channel_id=1, source_target_pairs={{0,1},{1,0},{2,3},{3,2},{4,5},{5,4},{6,7},{7,6},{8,9},{9,8},{10,11... | collective-permute-start | bytes 196616 | tf_op jit(solution)/shard_map/ppermute | solution.py:62
  12.2 1.8 %copy-start.5 = (f32[1536]{0:T(1024)S(1)}, f32[1536]{0:T(1024)}, u32[]{:S(2)}) copy-start(f32[1536]{0:T(1024)} %param.11) | copy-start | bytes 18436
  12.2 5.3 %collective-permute-start.4 = (f32[32,2048]{1,0:T(8,128)S(1)}, f32[32,2048]{1,0:T(8,128)S(1)}, u32[]{:S(2)}, u32[]{:S(2)}) collective-permute-start(f32[32,2048]{1,0:T(8,128)S(1)} %pad_maximum_fusion.refs_0_), channel_id=1, source_target_pairs={{0,2},{1,3},{2,0},{3,1},{4,6},{5,7},{6,4},{7,5},{8,10},{9,11},{10,... | collective-permute-start | bytes 786440 | tf_op jit(solution)/shard_map/ppermute | solution.py:62
  12.3 5.2 %collective-permute-start.5 = (f32[16,2048]{1,0:T(8,128)S(1)}, f32[16,2048]{1,0:T(8,128)S(1)}, u32[]{:S(2)}, u32[]{:S(2)}) collective-permute-start(f32[16,2048]{1,0:T(8,128)S(1)} %maximum_select_fusion.rows), channel_id=1, source_target_pairs={{0,6},{1,7},{2,4},{3,5},{4,2},{5,3},{6,0},{7,1},{8,14},{9,15},{10,... | collective-permute-start | bytes 393224 | tf_op jit(solution)/shard_map/ppermute | solution.py:62
  14.0 0.7 %copy-start = (f32[512]{0:T(512)S(1)}, f32[512]{0:T(512)}, u32[]{:S(2)}) copy-start(f32[512]{0:T(512)} %param.10) | copy-start | bytes 6148
  14.0 0.7 %copy-start.4 = (s32[1,16]{1,0:T(1,128)S(1)}, s32[1,16]{1,0:T(1,128)}, u32[]{:S(2)}) copy-start(s32[1,16]{1,0:T(1,128)} %live.1) | copy-start | bytes 196
  14.0 0.7 %copy-start.1 = (f32[2]{0:T(128)S(1)}, f32[2]{0:T(128)}, u32[]{:S(2)}) copy-start(f32[2]{0:T(128)} %tau.1) | copy-start | bytes 28
  14.0 0.7 %copy-start.2 = (f32[2]{0:T(128)S(1)}, f32[2]{0:T(128)}, u32[]{:S(2)}) copy-start(f32[2]{0:T(128)} %weight.1) | copy-start | bytes 28
  14.0 0.7 %copy-start.3 = (f32[2]{0:T(128)S(1)}, f32[2]{0:T(128)}, u32[]{:S(2)}) copy-start(f32[2]{0:T(128)} %frequency.1) | copy-start | bytes 28
  17.9 3.2 %collective-permute-start.6 = (f32[2,16,64]{2,1,0:T(8,128)S(1)}, f32[2,16,64]{2,1,0:T(8,128)S(1)}, u32[]{:S(2)}, u32[]{:S(2)}) collective-permute-start(f32[2,16,64]{2,1,0:T(8,128)S(1)} %there.1), channel_id=1, source_target_pairs={{0,6},{1,7},{2,4},{3,5},{4,2},{5,3},{6,0},{7,1},{8,14},{9,15},{10,... | collective-permute-start | bytes 24584 | tf_op jit(solution)/shard_map/ppermute | solution.py:226

commit v4 on v3

--- a/solution.py
+++ b/solution.py
@@ -9,7 +9,7 @@
 
 
 AXES = ("pts", "tau")
-DIRECT = 4
+CROSSING = ((1, 1),)
 VMEM = pl.BlockSpec(memory_space=pltpu.VMEM)
 PARAMS = pltpu.CompilerParams(vmem_limit_bytes=8 * 1024 * 1024)
 SMEM = pl.BlockSpec(memory_space=pltpu.SMEM)
@@ -34,11 +34,15 @@
 
 def direct(mesh, dim):
     size = layout(mesh)[dim]
-    return size <= DIRECT and size & (size - 1) == 0
+    return size in (1, 2, 4) and (dim != 3 or size < 4)
 
 
 def crossing(mesh, dim, step):
     return (dim, step) in CROSSING and layout(mesh)[2] == 2 and direct(mesh, dim)
+
+
+def ring(at):
+    return at ^ (at >> 1)
 
 
 def moves(mesh, dim, step):
@@ -46,7 +50,7 @@
     pairs = []
     for i in range(sizes[0] * strides_of(mesh)[0]):
         at = (i // stride) % sizes[dim]
-        to = i + ((at ^ step) - at) * stride
+        to = i + (ring((ring(at) + step) % sizes[dim]) - at) * stride
         if crossing(mesh, dim, step):
             to += (1 - 2 * ((to // sizes[3]) % 2)) * sizes[3]
         pairs.append((i, to))
@@ -135,7 +139,7 @@
     at_pair = lax.rem(lax.div(place, sizes[2]), sizes[1])
     far = lax.div(place, sizes[2] * sizes[1])
     if direct(mesh, 0):
-        step = far ^ far_mine
+        step = (ring(far_mine) - ring(far)) & (sizes[0] - 1)
         nth = jnp.where(step == 0, 0, sizes[0] - step)
         for k in range(1, sizes[0]):
             if crossing(mesh, 0, k):
@@ -192,10 +196,7 @@
         rows = jnp.roll(jnp.concatenate(row_blocks, 0), group * device_pts, axis=0)
     far_blocks = gather(mesh, 0, own)
     row_sets = gather(mesh, 1, rows)
-    pieces = [jnp.concatenate(far_blocks, axis=0)]
-    column_sets = []
-    for piece in pieces:
-        column_sets += gather(mesh, 2, piece)
+    column_sets = gather(mesh, 2, jnp.concatenate(far_blocks, axis=0))
 
     decay, mixing, mask = pl.pallas_call(
         prepare_kernel,
@@ -244,9 +245,6 @@
     return out.reshape(n_frequencies, n_rows, 1, mask.shape[1])
 
 
-CROSSING = ((0, 1), (1, 1))
-
-
 def solution(mesh):
     return jax.shard_map(
         functools.partial(on_device, mesh),

time: 22.1 us -> 22.6 us (1.023)
  waiting for transfers between devices: 7.6 us -> 8.5 us
  starting transfers between devices: 10.4 us -> 9.97 us
    ppermute x1, starting transfers between devices: 1.65 us -> 0.64 us  [on_device(): back.append(lax.ppermute(there, AXES, moves(mesh, 1, step)))]
    ppermute x1, waiting for transfers between devices: 1.1 us -> 2.11 us  [on_device(): back.append(lax.ppermute(there, AXES, moves(mesh, 1, step)))]
    ppermute x6, starting transfers between devices: 8.72 us -> 9.33 us  [gather(): blocks.append(lax.ppermute(block, AXES, moves(mesh, dim, step)))]
  transfers between devices with their start and end apart: 7 -> 7, of which waited for: 4 -> 5; matrix products, arithmetic and copies ran while one was open for 0% -> 0% of each run, Pallas kernels for 5% -> 5%
where the time goes in v4:
time: 22.6 us; the launch traced here: 22.4 us
  starting transfers between devices  9.97 us (44%)
  waiting for transfers between devices  8.5 us (38%)
  Pallas kernels  2.31 us (10%)
  other arithmetic  0.83 us (4%)
  local copies, waits for them, and re-layouts  0.69 us (3%)
    ppermute x6, starting transfers between devices, gather(): blocks.append(lax.ppermute(block, AXES, moves(mesh, dim, step)))  9.33 us
    ppermute x6, waiting for transfers between devices, gather(): blocks.append(lax.ppermute(block, AXES, moves(mesh, dim, step)))  6.39 us
    ppermute x1, waiting for transfers between devices, on_device(): back.append(lax.ppermute(there, AXES, moves(mesh, 1, step)))  2.11 us
    add x1, other arithmetic, on_device(): jnp.pad(occupied_values, ((0, 0), (0, n_all - n_occupied)))  0.81 us
    pallas_call x1, Pallas kernels, on_device(): pl.pallas_call(functools.partial(join_kernel, mesh, device_pts), name='jo...  0.78 us
    pallas_call x1, Pallas kernels, on_device(): pl.pallas_call(prepare_kernel, name='prepare', out_shape=[jax.ShapeDtypeS...  0.7 us
    unnamed x12, local copies, waits for them, and re-layouts  0.69 us
    ppermute x1, starting transfers between devices, on_device(): back.append(lax.ppermute(there, AXES, moves(mesh, 1, step)))  0.64 us
  transfers between devices with their start and end apart: 7, of which 5 were waited for; matrix products, arithmetic and copies ran while one was open for 0% of the time, Pallas kernels for 5%

profile of v4, /device:TPU:0, one launch (start us, length us, event | category | flops | bytes accessed | tf_op | source)
XLA Modules:
  0.0 22.4 jit_solution(1553344937511504704)
XLA Ops:
  0.0 0.8 %pad_add_fusion = f32[8,2048]{1,0:T(8,128)S(1)} fusion(f32[8,1536]{1,0:T(8,128)} %param.9, f32[8,512]{1,0:T(8,128)} %param.8), kind=kLoop, calls=%fused_computation.2 | loop fusion | flops 16384 | bytes 131072 | tf_op jit(solution)/shard_map/add | solution.py:190
  0.8 3.1 %collective-permute-start.3 = (f32[8,2048]{1,0:T(8,128)S(1)}, f32[8,2048]{1,0:T(8,128)S(1)}, u32[]{:S(2)}, u32[]{:S(2)}) collective-permute-start(f32[8,2048]{1,0:T(8,128)S(1)} %pad_add_fusion), channel_id=1, source_target_pairs={{0,8},{1,9},{2,10},{3,11},{4,12},{5,13},{6,14},{7,15},{8,24},{9,25... | collective-permute-start | bytes 196616 | tf_op jit(solution)/shard_map/ppermute | solution.py:66
  3.9 2.5 %collective-permute-start.2 = (f32[8,2048]{1,0:T(8,128)S(1)}, f32[8,2048]{1,0:T(8,128)S(1)}, u32[]{:S(2)}, u32[]{:S(2)}) collective-permute-start(f32[8,2048]{1,0:T(8,128)S(1)} %pad_add_fusion), channel_id=1, source_target_pairs={{0,24},{1,25},{2,26},{3,27},{4,28},{5,29},{6,30},{7,31},{8,16},{9,... | collective-permute-start | bytes 196616 | tf_op jit(solution)/shard_map/ppermute | solution.py:66
  6.3 1.6 %collective-permute-start.1 = (f32[8,2048]{1,0:T(8,128)S(1)}, f32[8,2048]{1,0:T(8,128)S(1)}, u32[]{:S(2)}, u32[]{:S(2)}) collective-permute-start(f32[8,2048]{1,0:T(8,128)S(1)} %pad_add_fusion), channel_id=1, source_target_pairs={{0,16},{1,17},{2,18},{3,19},{4,20},{5,21},{6,22},{7,23},{8,0},{9,1... | collective-permute-start | bytes 196616 | tf_op jit(solution)/shard_map/ppermute | solution.py:66
  7.9 1.5 %collective-permute-start = (f32[8,2048]{1,0:T(8,128)S(1)}, f32[8,2048]{1,0:T(8,128)S(1)}, u32[]{:S(2)}, u32[]{:S(2)}) collective-permute-start(f32[8,2048]{1,0:T(8,128)S(1)} %pad_add_fusion), channel_id=1, source_target_pairs={{0,1},{1,0},{2,3},{3,2},{4,5},{5,4},{6,7},{7,6},{8,9},{9,8},{10,11... | collective-permute-start | bytes 196616 | tf_op jit(solution)/shard_map/ppermute | solution.py:66
  9.4 1.4 %collective-permute-done.2 = f32[8,2048]{1,0:T(8,128)S(1)} collective-permute-done((f32[8,2048]{1,0:T(8,128)S(1)}, f32[8,2048]{1,0:T(8,128)S(1)}, u32[]{:S(2)}, u32[]{:S(2)}) %collective-permute-start.2) | collective-permute-done | bytes 65568 | tf_op jit(solution)/shard_map/ppermute | solution.py:66
  10.8 0.2 %collective-permute-done.1 = f32[8,2048]{1,0:T(8,128)S(1)} collective-permute-done((f32[8,2048]{1,0:T(8,128)S(1)}, f32[8,2048]{1,0:T(8,128)S(1)}, u32[]{:S(2)}, u32[]{:S(2)}) %collective-permute-start.1) | collective-permute-done | bytes 65568 | tf_op jit(solution)/shard_map/ppermute | solution.py:66
  11.1 0.0 copy-start.5
  11.1 0.1 collective-permute-start.4
  11.2 1.0 %collective-permute-done = f32[8,2048]{1,0:T(8,128)S(1)} collective-permute-done((f32[8,2048]{1,0:T(8,128)S(1)}, f32[8,2048]{1,0:T(8,128)S(1)}, u32[]{:S(2)}, u32[]{:S(2)}) %collective-permute-start) | collective-permute-done | bytes 65568 | tf_op jit(solution)/shard_map/ppermute | solution.py:66
  12.2 0.6 %collective-permute-start.5 = (f32[16,2048]{1,0:T(8,128)S(1)}, f32[16,2048]{1,0:T(8,128)S(1)}, u32[]{:S(2)}, u32[]{:S(2)}) collective-permute-start(f32[16,2048]{1,0:T(8,128)S(1)} %maximum_select_fusion.rows), channel_id=1, source_target_pairs={{0,6},{1,7},{2,4},{3,5},{4,2},{5,3},{6,0},{7,1},{8,14},{9,15},{10,... | collective-permute-start | bytes 393224 | tf_op jit(solution)/shard_map/ppermute | solution.py:66
  12.8 0.0 copy-start.1
  12.9 0.0 copy-start.2
  12.9 0.0 copy-start.3
  12.9 0.6 %copy-done = f32[512]{0:T(512)S(1)} copy-done((f32[512]{0:T(512)S(1)}, f32[512]{0:T(512)}, u32[]{:S(2)}) %copy-start) | copy-done | bytes 2072
  13.5 0.0 copy-done.2
  13.5 0.0 copy-done.3
  13.6 0.7 %prepare.1 = (f32[2,2048]{1,0:T(2,128)S(1)}, f32[4,128]{1,0:T(4,128)S(1)}, f32[8,128]{1,0:T(8,128)S(1)}) custom-call(f32[2]{0:T(128)S(1)} %copy-done.1, f32[2]{0:T(128)S(1)} %copy-done.2, f32[2]{0:T(128)S(1)} %copy-done.3, f32[1,512]{1,0:T(1,128)S(1)} %bitcast.4, f32[1,1536]{1,0:T(1,128)S(1)} %broadcast_in_dim.7.virtual_energy, s32[1,16]{1,0:T(1,128)S(1)} %copy-done.4), custom_call_target="tpu_custom_call" | custom-call | tf_op jit(solution)/shard_map/prepare/pallas_call | solution.py:201
  14.2 3.8 %collective-permute-done.5.rows = f32[16,2048]{1,0:T(8,128)S(1)} collective-permute-done((f32[16,2048]{1,0:T(8,128)S(1)}, f32[16,2048]{1,0:T(8,128)S(1)}, u32[]{:S(2)}, u32[]{:S(2)}) %collective-permute-start.5) | collective-permute-done | bytes 131104 | tf_op jit(solution)/shard_map/ppermute | solution.py:66
  18.0 0.3 %there.1 = f32[2,16,64]{2,1,0:T(8,128)S(1)} custom-call(f32[16,2048]{1,0:T(8,128)S(1)} %collective-permute-done.5.rows, f32[32,2048]{1,0:T(8,128)S(1)} %pad_maximum_fusion.refs_0_, f32[32,2048]{1,0:T(8,128)S(1)} %collective-permute-done.4.refs_1_, f32[2,2048]{1,0:T(2,128)S(1)} %get-tuple-element.8.refs_2_, f32[4,128]{1,0:T(4,128)S(1)} %get-tuple-element.9.refs_3_), custom_call_target="tpu_custom_call" | custom-call | flops 25165824 | bytes 655360 | tf_op jit(solution)/shard_map/there/pallas_call | solution.py:218
  18.4 0.6 %collective-permute-start.6 = (f32[2,16,64]{2,1,0:T(8,128)S(1)}, f32[2,16,64]{2,1,0:T(8,128)S(1)}, u32[]{:S(2)}, u32[]{:S(2)}) collective-permute-start(f32[2,16,64]{2,1,0:T(8,128)S(1)} %there.1), channel_id=1, source_target_pairs={{0,6},{1,7},{2,4},{3,5},{4,2},{5,3},{6,0},{7,1},{8,14},{9,15},{10,... | collective-permute-start | bytes 24584 | tf_op jit(solution)/shard_map/ppermute | solution.py:227
  19.0 0.5 %here.1 = f32[32,128]{1,0:T(8,128)S(1)} custom-call(f32[16,2048]{1,0:T(8,128)S(1)} %maximum_select_fusion.rows, f32[32,2048]{1,0:T(8,128)S(1)} %pad_maximum_fusion.refs_0_, f32[32,2048]{1,0:T(8,128)S(1)} %collective-permute-done.4.refs_1_, f32[2,2048]{1,0:T(2,128)S(1)} %get-tuple-element.8.refs_2_, f32[4,128]{1,0:T(4,128)S(1)} %get-tuple-element.9.refs_3_, ...), custom_call_target="tpu_custom_call" | custom-call | flops 25165824 | bytes 655360 | tf_op jit(solution)/shard_map/here/pallas_call | solution.py:228
  19.5 2.1 %collective-permute-done.6.refs_0_ = f32[2,16,64]{2,1,0:T(8,128)S(1)} collective-permute-done((f32[2,16,64]{2,1,0:T(8,128)S(1)}, f32[2,16,64]{2,1,0:T(8,128)S(1)}, u32[]{:S(2)}, u32[]{:S(2)}) %collective-permute-start.6) | collective-permute-done | bytes 8224 | tf_op jit(solution)/shard_map/ppermute | solution.py:227
  21.6 0.8 %join.1 = f32[32,128]{1,0:T(8,128)} custom-call(f32[32,128]{1,0:T(8,128)S(1)} %here.1, f32[8,128]{1,0:T(8,128)S(1)} %get-tuple-element.10.refs_4_.mask, f32[2,16,64]{2,1,0:T(8,128)S(1)} %collective-permute-done.6.refs_0_), custom_call_target="tpu_custom_call" | custom-call | tf_op jit(solution)/shard_map/join/pallas_call | solution.py:237
  (10 shorter events, 0.0 us)
Async XLA Ops:
  0.8 8.6 %collective-permute-start.3 = (f32[8,2048]{1,0:T(8,128)S(1)}, f32[8,2048]{1,0:T(8,128)S(1)}, u32[]{:S(2)}, u32[]{:S(2)}) collective-permute-start(f32[8,2048]{1,0:T(8,128)S(1)} %pad_add_fusion), channel_id=1, source_target_pairs={{0,8},{1,9},{2,10},{3,11},{4,12},{5,13},{6,14},{7,15},{8,24},{9,25... | collective-permute-start | bytes 196616 | tf_op jit(solution)/shard_map/ppermute | solution.py:66
  3.9 7.0 %collective-permute-start.2 = (f32[8,2048]{1,0:T(8,128)S(1)}, f32[8,2048]{1,0:T(8,128)S(1)}, u32[]{:S(2)}, u32[]{:S(2)}) collective-permute-start(f32[8,2048]{1,0:T(8,128)S(1)} %pad_add_fusion), channel_id=1, source_target_pairs={{0,24},{1,25},{2,26},{3,27},{4,28},{5,29},{6,30},{7,31},{8,16},{9,... | collective-permute-start | bytes 196616 | tf_op jit(solution)/shard_map/ppermute | solution.py:66
  6.3 4.7 %collective-permute-start.1 = (f32[8,2048]{1,0:T(8,128)S(1)}, f32[8,2048]{1,0:T(8,128)S(1)}, u32[]{:S(2)}, u32[]{:S(2)}) collective-permute-start(f32[8,2048]{1,0:T(8,128)S(1)} %pad_add_fusion), channel_id=1, source_target_pairs={{0,16},{1,17},{2,18},{3,19},{4,20},{5,21},{6,22},{7,23},{8,0},{9,1... | collective-permute-start | bytes 196616 | tf_op jit(solution)/shard_map/ppermute | solution.py:66
  7.9 4.3 %collective-permute-start = (f32[8,2048]{1,0:T(8,128)S(1)}, f32[8,2048]{1,0:T(8,128)S(1)}, u32[]{:S(2)}, u32[]{:S(2)}) collective-permute-start(f32[8,2048]{1,0:T(8,128)S(1)} %pad_add_fusion), channel_id=1, source_target_pairs={{0,1},{1,0},{2,3},{3,2},{4,5},{5,4},{6,7},{7,6},{8,9},{9,8},{10,11... | collective-permute-start | bytes 196616 | tf_op jit(solution)/shard_map/ppermute | solution.py:66
  11.1 1.8 %copy-start.5 = (f32[1536]{0:T(1024)S(1)}, f32[1536]{0:T(1024)}, u32[]{:S(2)}) copy-start(f32[1536]{0:T(1024)} %param.11) | copy-start | bytes 18436
  11.1 6.9 %collective-permute-start.4 = (f32[32,2048]{1,0:T(8,128)S(1)}, f32[32,2048]{1,0:T(8,128)S(1)}, u32[]{:S(2)}, u32[]{:S(2)}) collective-permute-start(f32[32,2048]{1,0:T(8,128)S(1)} %pad_maximum_fusion.refs_0_), channel_id=1, source_target_pairs={{0,2},{1,3},{2,0},{3,1},{4,6},{5,7},{6,4},{7,5},{8,10},{9,11},{10,... | collective-permute-start | bytes 786440 | tf_op jit(solution)/shard_map/ppermute | solution.py:66
  12.2 5.8 %collective-permute-start.5 = (f32[16,2048]{1,0:T(8,128)S(1)}, f32[16,2048]{1,0:T(8,128)S(1)}, u32[]{:S(2)}, u32[]{:S(2)}) collective-permute-start(f32[16,2048]{1,0:T(8,128)S(1)} %maximum_select_fusion.rows), channel_id=1, source_target_pairs={{0,6},{1,7},{2,4},{3,5},{4,2},{5,3},{6,0},{7,1},{8,14},{9,15},{10,... | collective-permute-start | bytes 393224 | tf_op jit(solution)/shard_map/ppermute | solution.py:66
  12.8 0.7 %copy-start = (f32[512]{0:T(512)S(1)}, f32[512]{0:T(512)}, u32[]{:S(2)}) copy-start(f32[512]{0:T(512)} %param.10) | copy-start | bytes 6148
  12.8 0.7 %copy-start.4 = (s32[1,16]{1,0:T(1,128)S(1)}, s32[1,16]{1,0:T(1,128)}, u32[]{:S(2)}) copy-start(s32[1,16]{1,0:T(1,128)} %live.1) | copy-start | bytes 196
  12.8 0.7 %copy-start.1 = (f32[2]{0:T(128)S(1)}, f32[2]{0:T(128)}, u32[]{:S(2)}) copy-start(f32[2]{0:T(128)} %tau.1) | copy-start | bytes 28
  12.9 0.7 %copy-start.2 = (f32[2]{0:T(128)S(1)}, f32[2]{0:T(128)}, u32[]{:S(2)}) copy-start(f32[2]{0:T(128)} %weight.1) | copy-start | bytes 28
  12.9 0.7 %copy-start.3 = (f32[2]{0:T(128)S(1)}, f32[2]{0:T(128)}, u32[]{:S(2)}) copy-start(f32[2]{0:T(128)} %frequency.1) | copy-start | bytes 28
  18.4 3.2 %collective-permute-start.6 = (f32[2,16,64]{2,1,0:T(8,128)S(1)}, f32[2,16,64]{2,1,0:T(8,128)S(1)}, u32[]{:S(2)}, u32[]{:S(2)}) collective-permute-start(f32[2,16,64]{2,1,0:T(8,128)S(1)} %there.1), channel_id=1, source_target_pairs={{0,6},{1,7},{2,4},{3,5},{4,2},{5,3},{6,0},{7,1},{8,14},{9,15},{10,... | collective-permute-start | bytes 24584 | tf_op jit(solution)/shard_map/ppermute | solution.py:227

commit v5 on v4

--- a/solution.py
+++ b/solution.py
@@ -86,7 +86,7 @@
     return dot(a, b) + (dot(a, b_low) + dot(a_low, b))
 
 
-def prepare_kernel(tau, weight, frequency, occupied_energy, virtual_energy, live, decay, mixing, mask):
+def prepare_kernel(mesh, device_pts, tau, weight, frequency, occupied_energy, virtual_energy, live, decay, mixing, mask, spread):
     n_occupied = occupied_energy.shape[1]
     for t in range(tau.shape[0]):
         decay[t : t + 1, :n_occupied] = jnp.exp(occupied_energy[...] * tau[t])
@@ -98,9 +98,11 @@
     width, blocks = mask.shape[1], live.shape[1]
     column = lax.broadcasted_iota(jnp.int32, (blocks, width), 1)
     block = lax.broadcasted_iota(jnp.int32, (blocks, width), 0)
-    spread = jnp.where(lax.div(column, width // blocks) == block, 1.0, 0.0)
+    repeat = jnp.where(lax.div(column, width // blocks) == block, 1.0, 0.0)
     marks = jnp.broadcast_to(live[...].astype(jnp.float32), (8, blocks))
-    mask[...] = jnp.dot(marks, spread, preferred_element_type=jnp.float32)
+    mask[...] = jnp.dot(marks, repeat, preferred_element_type=jnp.float32)
+    _, pair, core, _ = coordinates(mesh)
+    spread[...] = spread_of(mesh, device_pts, pair, core, spread.shape[0], width).astype(jnp.bfloat16)
 
 
 def chi_parts(n_occupied, rows, columns, decay, mixing, n_frequencies):
@@ -121,12 +123,6 @@
             total = term if total is None else total + term
         out.append(total)
     return out
-
-
-def there_kernel(n_occupied, n_frequencies, rows, *refs):
-    columns, (decay, mixing, out) = refs[:-3], refs[-3:]
-    for k, chi in enumerate(chi_parts(n_occupied, rows, columns, decay, mixing, n_frequencies)):
-        out[k] = chi
 
 
 def spread_of(mesh, device_pts, pair, core, width, here):
@@ -150,23 +146,15 @@
     return jnp.where((source == row) & (at_pair == pair), 1.0, 0.0)
 
 
-def here_kernel(mesh, n_occupied, n_frequencies, device_pts, rows, *refs):
-    columns, (decay, mixing, mask, out) = refs[:-4], refs[-4:]
+def chi_kernel(n_occupied, n_frequencies, rows, *refs):
+    columns, (decay, mixing, spread, out) = refs[:-4], refs[-4:]
     chi = jnp.concatenate(chi_parts(n_occupied, rows, columns, decay, mixing, n_frequencies), axis=0)
-    _, pair, core, _ = coordinates(mesh)
-    spread = spread_of(mesh, device_pts, pair, core, chi.shape[1], out.shape[1])
-    out[...] = jnp.dot(chi, spread, precision=lax.Precision.HIGHEST, preferred_element_type=jnp.float32) * mask[0:1, :]
-
-
-def join_kernel(mesh, device_pts, here, mask, *refs):
-    back, out = refs[:-1], refs[-1]
-    total = here[...]
-    _, pair, core, _ = coordinates(mesh)
-    for step, came in enumerate(back, 1):
-        chi = came[...].reshape(-1, came.shape[2])
-        spread = spread_of(mesh, device_pts, pair ^ step, 1 - core if crossing(mesh, 1, step) else core, chi.shape[1], out.shape[1])
-        moved = jnp.dot(chi, spread, precision=lax.Precision.HIGHEST, preferred_element_type=jnp.float32)
-        total = total + moved * mask[0:1, :]
+    total = None
+    for _ in range(3):
+        part = chi.astype(jnp.bfloat16)
+        chi = chi - part.astype(jnp.float32)
+        moved = jnp.dot(part, spread[...], preferred_element_type=jnp.float32)
+        total = moved if total is None else total + moved
     out[...] = total
 
 
@@ -198,50 +186,38 @@
     row_sets = gather(mesh, 1, rows)
     column_sets = gather(mesh, 2, jnp.concatenate(far_blocks, axis=0))
 
-    decay, mixing, mask = pl.pallas_call(
-        prepare_kernel,
+    decay, mixing, mask, spread = pl.pallas_call(
+        functools.partial(prepare_kernel, mesh, device_pts),
         name="prepare",
         out_shape=[
             jax.ShapeDtypeStruct((n_times, n_all), f32),
             jax.ShapeDtypeStruct((n_times * n_frequencies, 128), f32),
             jax.ShapeDtypeStruct((8, far * pairs * cores * device_pts), f32),
+            jax.ShapeDtypeStruct((far * cores * device_pts, far * pairs * cores * device_pts), jnp.bfloat16),
         ],
         in_specs=[SMEM] * 3 + [VMEM] * 3,
-        out_specs=[VMEM] * 3,
+        out_specs=[VMEM] * 4,
         compiler_params=PARAMS,
     )(tau_points, tau_weights, frequencies, occupied_energy[None], virtual_energy[None], pair_live)
 
     n_rows, width = rows.shape[0], far * cores * device_pts
     cost = pl.CostEstimate(flops=6 * n_times * n_rows * width * n_all, bytes_accessed=4 * n_all * (width + n_rows), transcendentals=0)
-    back = []
-    for step in range(1, pairs):
-        there = pl.pallas_call(
-            functools.partial(there_kernel, n_occupied, n_frequencies),
-            name="there",
-            out_shape=jax.ShapeDtypeStruct((n_frequencies, n_rows, width), f32),
-            in_specs=[VMEM] * (3 + len(column_sets)),
+
+    def chi_of(part):
+        return pl.pallas_call(
+            functools.partial(chi_kernel, n_occupied, n_frequencies),
+            out_shape=jax.ShapeDtypeStruct((n_frequencies * n_rows, mask.shape[1]), f32),
+            in_specs=[VMEM] * (4 + len(column_sets)),
             out_specs=VMEM,
             cost_estimate=cost,
             compiler_params=PARAMS,
-        )(row_sets[step], *column_sets, decay, mixing)
+        )(part, *column_sets, decay, mixing, spread)
+
+    back = []
+    for step in range(1, pairs):
+        there = chi_of(row_sets[step])
         back.append(lax.ppermute(there, AXES, moves(mesh, 1, step)))
-    here = pl.pallas_call(
-        functools.partial(here_kernel, mesh, n_occupied, n_frequencies, device_pts),
-        name="here",
-        out_shape=jax.ShapeDtypeStruct((n_frequencies * n_rows, mask.shape[1]), f32),
-        in_specs=[VMEM] * (4 + len(column_sets)),
-        out_specs=VMEM,
-        cost_estimate=cost,
-        compiler_params=PARAMS,
-    )(rows, *column_sets, decay, mixing, mask)
-    out = pl.pallas_call(
-        functools.partial(join_kernel, mesh, device_pts),
-        name="join",
-        out_shape=jax.ShapeDtypeStruct((n_frequencies * n_rows, mask.shape[1]), f32),
-        in_specs=[VMEM] * (2 + len(back)),
-        out_specs=VMEM,
-        compiler_params=PARAMS,
-    )(here, mask, *back)
+    out = (chi_of(rows) + sum(back)) * mask[0:1, :]
     return out.reshape(n_frequencies, n_rows, 1, mask.shape[1])
 
 

time: 22.6 us -> 22.5 us (level)
  Pallas kernels: 2.31 us -> 1.67 us
  other arithmetic: 0.83 us -> 1.44 us
    pallas_call x4 -> x3, Pallas kernels: 2.31 us -> 1.67 us  [the longest x2 0.97 us: chi_of(): pl.pallas_call(functools.partial(chi_kernel, n_occupied, n_frequencies),...]
    mul x0 -> x1, other arithmetic: none -> 0.61 us  [on_device(): out = (chi_of(rows) + sum(back)) * mask[0:1, :]]
where the time goes in v5:
time: 22.5 us; the launch traced here: 22.3 us
  starting transfers between devices  9.91 us (44%)
  waiting for transfers between devices  8.49 us (38%)
  Pallas kernels  1.67 us (7%)
  other arithmetic  1.44 us (6%)
  local copies, waits for them, and re-layouts  0.7 us (3%)
    ppermute x6, starting transfers between devices, gather(): blocks.append(lax.ppermute(block, AXES, moves(mesh, dim, step)))  9.33 us
    ppermute x6, waiting for transfers between devices, gather(): blocks.append(lax.ppermute(block, AXES, moves(mesh, dim, step)))  6.39 us
    ppermute x1, waiting for transfers between devices, on_device(): back.append(lax.ppermute(there, AXES, moves(mesh, 1, step)))  2.1 us
    pallas_call x2, Pallas kernels, chi_of(): pl.pallas_call(functools.partial(chi_kernel, n_occupied, n_frequencies),...  0.97 us
    add x1, other arithmetic, on_device(): jnp.pad(occupied_values, ((0, 0), (0, n_all - n_occupied)))  0.81 us
    pallas_call x1, Pallas kernels, on_device(): pl.pallas_call(functools.partial(prepare_kernel, mesh, device_pts), name=...  0.7 us
    unnamed x12, local copies, waits for them, and re-layouts  0.69 us
    mul x1, other arithmetic, on_device(): out = (chi_of(rows) + sum(back)) * mask[0:1, :]  0.61 us
  transfers between devices with their start and end apart: 7, of which 5 were waited for; matrix products, arithmetic and copies ran while one was open for 0% of the time, Pallas kernels for 5%

profile of v5, /device:TPU:0, one launch (start us, length us, event | category | flops | bytes accessed | tf_op | source)
XLA Modules:
  0.0 22.3 jit_solution(2577061007884514200)
XLA Ops:
  0.0 0.8 %pad_add_fusion = f32[8,2048]{1,0:T(8,128)S(1)} fusion(f32[8,1536]{1,0:T(8,128)} %param.9, f32[8,512]{1,0:T(8,128)} %param.8), kind=kLoop, calls=%fused_computation.2 | loop fusion | flops 16384 | bytes 131072 | tf_op jit(solution)/shard_map/add | solution.py:178
  0.8 3.1 %collective-permute-start.3 = (f32[8,2048]{1,0:T(8,128)S(1)}, f32[8,2048]{1,0:T(8,128)S(1)}, u32[]{:S(2)}, u32[]{:S(2)}) collective-permute-start(f32[8,2048]{1,0:T(8,128)S(1)} %pad_add_fusion), channel_id=1, source_target_pairs={{0,8},{1,9},{2,10},{3,11},{4,12},{5,13},{6,14},{7,15},{8,24},{9,25... | collective-permute-start | bytes 196616 | tf_op jit(solution)/shard_map/ppermute | solution.py:66
  3.9 2.5 %collective-permute-start.2 = (f32[8,2048]{1,0:T(8,128)S(1)}, f32[8,2048]{1,0:T(8,128)S(1)}, u32[]{:S(2)}, u32[]{:S(2)}) collective-permute-start(f32[8,2048]{1,0:T(8,128)S(1)} %pad_add_fusion), channel_id=1, source_target_pairs={{0,24},{1,25},{2,26},{3,27},{4,28},{5,29},{6,30},{7,31},{8,16},{9,... | collective-permute-start | bytes 196616 | tf_op jit(solution)/shard_map/ppermute | solution.py:66
  6.3 1.6 %collective-permute-start.1 = (f32[8,2048]{1,0:T(8,128)S(1)}, f32[8,2048]{1,0:T(8,128)S(1)}, u32[]{:S(2)}, u32[]{:S(2)}) collective-permute-start(f32[8,2048]{1,0:T(8,128)S(1)} %pad_add_fusion), channel_id=1, source_target_pairs={{0,16},{1,17},{2,18},{3,19},{4,20},{5,21},{6,22},{7,23},{8,0},{9,1... | collective-permute-start | bytes 196616 | tf_op jit(solution)/shard_map/ppermute | solution.py:66
  7.9 1.5 %collective-permute-start = (f32[8,2048]{1,0:T(8,128)S(1)}, f32[8,2048]{1,0:T(8,128)S(1)}, u32[]{:S(2)}, u32[]{:S(2)}) collective-permute-start(f32[8,2048]{1,0:T(8,128)S(1)} %pad_add_fusion), channel_id=1, source_target_pairs={{0,1},{1,0},{2,3},{3,2},{4,5},{5,4},{6,7},{7,6},{8,9},{9,8},{10,11... | collective-permute-start | bytes 196616 | tf_op jit(solution)/shard_map/ppermute | solution.py:66
  9.4 1.4 %collective-permute-done.2 = f32[8,2048]{1,0:T(8,128)S(1)} collective-permute-done((f32[8,2048]{1,0:T(8,128)S(1)}, f32[8,2048]{1,0:T(8,128)S(1)}, u32[]{:S(2)}, u32[]{:S(2)}) %collective-permute-start.2) | collective-permute-done | bytes 65568 | tf_op jit(solution)/shard_map/ppermute | solution.py:66
  10.8 0.2 %collective-permute-done.1 = f32[8,2048]{1,0:T(8,128)S(1)} collective-permute-done((f32[8,2048]{1,0:T(8,128)S(1)}, f32[8,2048]{1,0:T(8,128)S(1)}, u32[]{:S(2)}, u32[]{:S(2)}) %collective-permute-start.1) | collective-permute-done | bytes 65568 | tf_op jit(solution)/shard_map/ppermute | solution.py:66
  11.1 0.0 copy-start.5
  11.1 0.1 collective-permute-start.4
  11.2 1.0 %collective-permute-done = f32[8,2048]{1,0:T(8,128)S(1)} collective-permute-done((f32[8,2048]{1,0:T(8,128)S(1)}, f32[8,2048]{1,0:T(8,128)S(1)}, u32[]{:S(2)}, u32[]{:S(2)}) %collective-permute-start) | collective-permute-done | bytes 65568 | tf_op jit(solution)/shard_map/ppermute | solution.py:66
  12.2 0.6 %collective-permute-start.5 = (f32[16,2048]{1,0:T(8,128)S(1)}, f32[16,2048]{1,0:T(8,128)S(1)}, u32[]{:S(2)}, u32[]{:S(2)}) collective-permute-start(f32[16,2048]{1,0:T(8,128)S(1)} %maximum_select_fusion.rows), channel_id=1, source_target_pairs={{0,6},{1,7},{2,4},{3,5},{4,2},{5,3},{6,0},{7,1},{8,14},{9,15},{10,... | collective-permute-start | bytes 393224 | tf_op jit(solution)/shard_map/ppermute | solution.py:66
  12.8 0.0 copy-start.1
  12.9 0.0 copy-start.2
  12.9 0.0 copy-start.3
  12.9 0.6 %copy-done = f32[512]{0:T(512)S(1)} copy-done((f32[512]{0:T(512)S(1)}, f32[512]{0:T(512)}, u32[]{:S(2)}) %copy-start) | copy-done | bytes 2072
  13.5 0.0 copy-done.2
  13.5 0.0 copy-done.3
  13.6 0.7 %prepare.1 = (f32[2,2048]{1,0:T(2,128)S(1)}, f32[4,128]{1,0:T(4,128)S(1)}, f32[8,128]{1,0:T(8,128)S(1)}, bf16[64,128]{1,0:T(8,128)(2,1)S(1)}) custom-call(f32[2]{0:T(128)S(1)} %copy-done.1, f32[2]{0:T(128)S(1)} %copy-done.2, f32[2]{0:T(128)S(1)} %copy-done.3, f32[1,512]{1,0:T(1,128)S(1)} %bitcast.6, f32[1,1536]{1,0:T(1,128)S(1)} %broadcast_in_dim.7.virtual_energy, ...), custom_call_target="tpu_custom_call" | custom-call | tf_op jit(solution)/shard_map/prepare/pallas_call | solution.py:189
  14.2 3.8 %collective-permute-done.5.rows = f32[16,2048]{1,0:T(8,128)S(1)} collective-permute-done((f32[16,2048]{1,0:T(8,128)S(1)}, f32[16,2048]{1,0:T(8,128)S(1)}, u32[]{:S(2)}, u32[]{:S(2)}) %collective-permute-start.5) | collective-permute-done | bytes 131104 | tf_op jit(solution)/shard_map/ppermute | solution.py:66
  18.0 0.5 %shard_map.83 = f32[32,128]{1,0:T(8,128)S(1)} custom-call(f32[16,2048]{1,0:T(8,128)S(1)} %collective-permute-done.5.rows, f32[32,2048]{1,0:T(8,128)S(1)} %pad_maximum_fusion.refs_0_, f32[32,2048]{1,0:T(8,128)S(1)} %collective-permute-done.4.refs_1_, f32[2,2048]{1,0:T(2,128)S(1)} %get-tuple-element.9.refs_2_, f32[4,128]{1,0:T(4,128)S(1)} %get-tuple-element.10.refs_3_, ...), custom_call_target="tpu_custom_call" | custom-call | flops 25165824 | bytes 655360 | tf_op jit(solution)/shard_map/pallas_call | solution.py:207
  18.5 0.6 %collective-permute-start.6 = (f32[32,128]{1,0:T(8,128)S(1)}, f32[32,128]{1,0:T(8,128)S(1)}, u32[]{:S(2)}, u32[]{:S(2)}) collective-permute-start(f32[32,128]{1,0:T(8,128)S(1)} %shard_map.83), channel_id=1, source_target_pairs={{0,6},{1,7},{2,4},{3,5},{4,2},{5,3},{6,0},{7,1},{8,14},{9,15},{10,... | collective-permute-start | bytes 49160 | tf_op jit(solution)/shard_map/ppermute | solution.py:219
  19.1 0.5 %shard_map.82 = f32[32,128]{1,0:T(8,128)S(1)} custom-call(f32[16,2048]{1,0:T(8,128)S(1)} %maximum_select_fusion.rows, f32[32,2048]{1,0:T(8,128)S(1)} %pad_maximum_fusion.refs_0_, f32[32,2048]{1,0:T(8,128)S(1)} %collective-permute-done.4.refs_1_, f32[2,2048]{1,0:T(2,128)S(1)} %get-tuple-element.9.refs_2_, f32[4,128]{1,0:T(4,128)S(1)} %get-tuple-element.10.refs_3_, ...), custom_call_target="tpu_custom_call" | custom-call | flops 25165824 | bytes 655360 | tf_op jit(solution)/shard_map/pallas_call | solution.py:207
  19.6 2.1 %collective-permute-done.6 = f32[32,128]{1,0:T(8,128)S(1)} collective-permute-done((f32[32,128]{1,0:T(8,128)S(1)}, f32[32,128]{1,0:T(8,128)S(1)}, u32[]{:S(2)}, u32[]{:S(2)}) %collective-permute-start.6) | collective-permute-done | bytes 16416 | tf_op jit(solution)/shard_map/ppermute | solution.py:219
  21.7 0.6 %add_multiply_fusion = f32[32,128]{1,0:T(8,128)} fusion(f32[32,128]{1,0:T(8,128)S(1)} %shard_map.82, f32[32,128]{1,0:T(8,128)S(1)} %collective-permute-done.6, f32[128]{0:T(128)S(1)} %slice_bitcast_fusion), kind=kLoop, calls=%fused_computation.3 | loop fusion | flops 8192 | bytes 49664 | tf_op jit(solution)/shard_map/mul | solution.py:220
  (11 shorter events, 0.1 us)
Async XLA Ops:
  0.8 8.6 %collective-permute-start.3 = (f32[8,2048]{1,0:T(8,128)S(1)}, f32[8,2048]{1,0:T(8,128)S(1)}, u32[]{:S(2)}, u32[]{:S(2)}) collective-permute-start(f32[8,2048]{1,0:T(8,128)S(1)} %pad_add_fusion), channel_id=1, source_target_pairs={{0,8},{1,9},{2,10},{3,11},{4,12},{5,13},{6,14},{7,15},{8,24},{9,25... | collective-permute-start | bytes 196616 | tf_op jit(solution)/shard_map/ppermute | solution.py:66
  3.9 7.0 %collective-permute-start.2 = (f32[8,2048]{1,0:T(8,128)S(1)}, f32[8,2048]{1,0:T(8,128)S(1)}, u32[]{:S(2)}, u32[]{:S(2)}) collective-permute-start(f32[8,2048]{1,0:T(8,128)S(1)} %pad_add_fusion), channel_id=1, source_target_pairs={{0,24},{1,25},{2,26},{3,27},{4,28},{5,29},{6,30},{7,31},{8,16},{9,... | collective-permute-start | bytes 196616 | tf_op jit(solution)/shard_map/ppermute | solution.py:66
  6.3 4.7 %collective-permute-start.1 = (f32[8,2048]{1,0:T(8,128)S(1)}, f32[8,2048]{1,0:T(8,128)S(1)}, u32[]{:S(2)}, u32[]{:S(2)}) collective-permute-start(f32[8,2048]{1,0:T(8,128)S(1)} %pad_add_fusion), channel_id=1, source_target_pairs={{0,16},{1,17},{2,18},{3,19},{4,20},{5,21},{6,22},{7,23},{8,0},{9,1... | collective-permute-start | bytes 196616 | tf_op jit(solution)/shard_map/ppermute | solution.py:66
  7.9 4.3 %collective-permute-start = (f32[8,2048]{1,0:T(8,128)S(1)}, f32[8,2048]{1,0:T(8,128)S(1)}, u32[]{:S(2)}, u32[]{:S(2)}) collective-permute-start(f32[8,2048]{1,0:T(8,128)S(1)} %pad_add_fusion), channel_id=1, source_target_pairs={{0,1},{1,0},{2,3},{3,2},{4,5},{5,4},{6,7},{7,6},{8,9},{9,8},{10,11... | collective-permute-start | bytes 196616 | tf_op jit(solution)/shard_map/ppermute | solution.py:66
  11.1 1.8 %copy-start.5 = (f32[1536]{0:T(1024)S(1)}, f32[1536]{0:T(1024)}, u32[]{:S(2)}) copy-start(f32[1536]{0:T(1024)} %param.11) | copy-start | bytes 18436
  11.1 6.9 %collective-permute-start.4 = (f32[32,2048]{1,0:T(8,128)S(1)}, f32[32,2048]{1,0:T(8,128)S(1)}, u32[]{:S(2)}, u32[]{:S(2)}) collective-permute-start(f32[32,2048]{1,0:T(8,128)S(1)} %pad_maximum_fusion.refs_0_), channel_id=1, source_target_pairs={{0,2},{1,3},{2,0},{3,1},{4,6},{5,7},{6,4},{7,5},{8,10},{9,11},{10,... | collective-permute-start | bytes 786440 | tf_op jit(solution)/shard_map/ppermute | solution.py:66
  12.2 5.8 %collective-permute-start.5 = (f32[16,2048]{1,0:T(8,128)S(1)}, f32[16,2048]{1,0:T(8,128)S(1)}, u32[]{:S(2)}, u32[]{:S(2)}) collective-permute-start(f32[16,2048]{1,0:T(8,128)S(1)} %maximum_select_fusion.rows), channel_id=1, source_target_pairs={{0,6},{1,7},{2,4},{3,5},{4,2},{5,3},{6,0},{7,1},{8,14},{9,15},{10,... | collective-permute-start | bytes 393224 | tf_op jit(solution)/shard_map/ppermute | solution.py:66
  12.8 0.7 %copy-start = (f32[512]{0:T(512)S(1)}, f32[512]{0:T(512)}, u32[]{:S(2)}) copy-start(f32[512]{0:T(512)} %param.10) | copy-start | bytes 6148
  12.8 0.7 %copy-start.4 = (s32[1,16]{1,0:T(1,128)S(1)}, s32[1,16]{1,0:T(1,128)}, u32[]{:S(2)}) copy-start(s32[1,16]{1,0:T(1,128)} %live.1) | copy-start | bytes 196
  12.8 0.7 %copy-start.1 = (f32[2]{0:T(128)S(1)}, f32[2]{0:T(128)}, u32[]{:S(2)}) copy-start(f32[2]{0:T(128)} %tau.1) | copy-start | bytes 28
  12.9 0.7 %copy-start.2 = (f32[2]{0:T(128)S(1)}, f32[2]{0:T(128)}, u32[]{:S(2)}) copy-start(f32[2]{0:T(128)} %weight.1) | copy-start | bytes 28
  12.9 0.7 %copy-start.3 = (f32[2]{0:T(128)S(1)}, f32[2]{0:T(128)}, u32[]{:S(2)}) copy-start(f32[2]{0:T(128)} %frequency.1) | copy-start | bytes 28
  18.5 3.2 %collective-permute-start.6 = (f32[32,128]{1,0:T(8,128)S(1)}, f32[32,128]{1,0:T(8,128)S(1)}, u32[]{:S(2)}, u32[]{:S(2)}) collective-permute-start(f32[32,128]{1,0:T(8,128)S(1)} %shard_map.83), channel_id=1, source_target_pairs={{0,6},{1,7},{2,4},{3,5},{4,2},{5,3},{6,0},{7,1},{8,14},{9,15},{10,... | collective-permute-start | bytes 49160 | tf_op jit(solution)/shard_map/ppermute | solution.py:219

commit v6 on v5

--- a/solution.py
+++ b/solution.py
@@ -79,11 +79,6 @@
 
 def dot(a, b):
     return lax.dot_general(a, b, (((1,), (1,)), ((), ())), preferred_element_type=jnp.float32)
-
-
-def products(left, right):
-    (a, a_low), (b, b_low) = halves(left), halves(right)
-    return dot(a, b) + (dot(a, b_low) + dot(a_low, b))
 
 
 def prepare_kernel(mesh, device_pts, tau, weight, frequency, occupied_energy, virtual_energy, live, decay, mixing, mask, spread):
@@ -105,14 +100,19 @@
     spread[...] = spread_of(mesh, device_pts, pair, core, spread.shape[0], width).astype(jnp.bfloat16)
 
 
-def chi_parts(n_occupied, rows, columns, decay, mixing, n_frequencies):
-    n_times = decay.shape[0]
+def scale_kernel(rows, decay, left, left_low):
+    left[...], left_low[...] = halves(jnp.concatenate([rows[...] * decay[t : t + 1, :] for t in range(decay.shape[0])], axis=0))
+
+
+def chi_parts(n_occupied, n_frequencies, left, left_low, columns, mixing):
     cols = jnp.concatenate([c[...] for c in columns], axis=0)
+    n_times = mixing.shape[0] // n_frequencies
     green = []
     for part in (slice(None, n_occupied), slice(n_occupied, None)):
-        left = jnp.concatenate([rows[:, part] * decay[t : t + 1, part] for t in range(n_times)], axis=0)
-        green.append(products(left, cols[:, part]))
-    n_rows = rows.shape[0]
+        right, right_low = halves(cols[:, part])
+        a, a_low = left[:, part], left_low[:, part]
+        green.append(dot(a, right) + (dot(a, right_low) + dot(a_low, right)))
+    n_rows = left.shape[0] // n_times
     pair = green[0] * green[1]
     out = []
     for k in range(n_frequencies):
@@ -146,9 +146,9 @@
     return jnp.where((source == row) & (at_pair == pair), 1.0, 0.0)
 
 
-def chi_kernel(n_occupied, n_frequencies, rows, *refs):
-    columns, (decay, mixing, spread, out) = refs[:-4], refs[-4:]
-    chi = jnp.concatenate(chi_parts(n_occupied, rows, columns, decay, mixing, n_frequencies), axis=0)
+def chi_kernel(n_occupied, n_frequencies, left, left_low, *refs):
+    columns, (mixing, spread, out) = refs[:-3], refs[-3:]
+    chi = jnp.concatenate(chi_parts(n_occupied, n_frequencies, left, left_low, columns, mixing), axis=0)
     total = None
     for _ in range(3):
         part = chi.astype(jnp.bfloat16)
@@ -204,6 +204,15 @@
     cost = pl.CostEstimate(flops=6 * n_times * n_rows * width * n_all, bytes_accessed=4 * n_all * (width + n_rows), transcendentals=0)
 
     def chi_of(part):
+        half = jax.ShapeDtypeStruct((n_times * n_rows, n_all), jnp.bfloat16)
+        left, left_low = pl.pallas_call(
+            scale_kernel,
+            name="scale",
+            out_shape=[half, half],
+            in_specs=[VMEM] * 2,
+            out_specs=[VMEM] * 2,
+            compiler_params=PARAMS,
+        )(part, decay)
         return pl.pallas_call(
             functools.partial(chi_kernel, n_occupied, n_frequencies),
             out_shape=jax.ShapeDtypeStruct((n_frequencies * n_rows, mask.shape[1]), f32),
@@ -211,7 +220,7 @@
             out_specs=VMEM,
             cost_estimate=cost,
             compiler_params=PARAMS,
-        )(part, *column_sets, decay, mixing, spread)
+        )(left, left_low, *column_sets, mixing, spread)
 
     back = []
     for step in range(1, pairs):

time: 22.5 us -> 22.1 us (0.982)
  waiting for transfers between devices: 8.49 us -> 6.87 us
  starting transfers between devices: 9.91 us -> 11 us
    ppermute x1, waiting for transfers between devices: 2.1 us -> 1.03 us  [on_device(): back.append(lax.ppermute(there, AXES, moves(mesh, 1, step)))]
    ppermute x1, starting transfers between devices: 0.58 us -> 1.59 us  [on_device(): back.append(lax.ppermute(there, AXES, moves(mesh, 1, step)))]
    ppermute x6, waiting for transfers between devices: 6.39 us -> 5.84 us  [gather(): blocks.append(lax.ppermute(block, AXES, moves(mesh, dim, step)))]
  transfers between devices with their start and end apart: 7 -> 7, of which waited for: 5 -> 4; matrix products, arithmetic and copies ran while one was open for 0% -> 0% of each run, Pallas kernels for 5% -> 6%
where the time goes in v6:
time: 22.1 us; the launch traced here: 21.9 us
  starting transfers between devices  11 us (50%)
  waiting for transfers between devices  6.87 us (31%)
  Pallas kernels  1.79 us (8%)
  other arithmetic  1.45 us (7%)
  local copies, waits for them, and re-layouts  0.7 us (3%)
    ppermute x6, starting transfers between devices, gather(): blocks.append(lax.ppermute(block, AXES, moves(mesh, dim, step)))  9.44 us
    ppermute x6, waiting for transfers between devices, gather(): blocks.append(lax.ppermute(block, AXES, moves(mesh, dim, step)))  5.84 us
    ppermute x1, starting transfers between devices, on_device(): back.append(lax.ppermute(there, AXES, moves(mesh, 1, step)))  1.59 us
    ppermute x1, waiting for transfers between devices, on_device(): back.append(lax.ppermute(there, AXES, moves(mesh, 1, step)))  1.03 us
    pallas_call x2, Pallas kernels, chi_of(): pl.pallas_call(functools.partial(chi_kernel, n_occupied, n_frequencies),...  1 us
    add x1, other arithmetic, on_device(): jnp.pad(occupied_values, ((0, 0), (0, n_all - n_occupied)))  0.81 us
    pallas_call x1, Pallas kernels, on_device(): pl.pallas_call(functools.partial(prepare_kernel, mesh, device_pts), name=...  0.7 us
    unnamed x12, local copies, waits for them, and re-layouts  0.69 us
  transfers between devices with their start and end apart: 7, of which 4 were waited for; matrix products, arithmetic and copies ran while one was open for 0% of the time, Pallas kernels for 6%

profile of v6, /device:TPU:0, one launch (start us, length us, event | category | flops | bytes accessed | tf_op | source)
XLA Modules:
  0.0 21.9 jit_solution(11732967372152329089)
XLA Ops:
  0.0 0.8 %pad_add_fusion = f32[8,2048]{1,0:T(8,128)S(1)} fusion(f32[8,1536]{1,0:T(8,128)} %param.9, f32[8,512]{1,0:T(8,128)} %param.8), kind=kLoop, calls=%fused_computation.2 | loop fusion | flops 16384 | bytes 131072 | tf_op jit(solution)/shard_map/add | solution.py:178
  0.8 4.1 %collective-permute-start.1 = (f32[8,2048]{1,0:T(8,128)S(1)}, f32[8,2048]{1,0:T(8,128)S(1)}, u32[]{:S(2)}, u32[]{:S(2)}) collective-permute-start(f32[8,2048]{1,0:T(8,128)S(1)} %pad_add_fusion), channel_id=1, source_target_pairs={{0,16},{1,17},{2,18},{3,19},{4,20},{5,21},{6,22},{7,23},{8,0},{9,1... | collective-permute-start | bytes 196616 | tf_op jit(solution)/shard_map/ppermute | solution.py:66
  4.9 1.3 %collective-permute-start.2 = (f32[8,2048]{1,0:T(8,128)S(1)}, f32[8,2048]{1,0:T(8,128)S(1)}, u32[]{:S(2)}, u32[]{:S(2)}) collective-permute-start(f32[8,2048]{1,0:T(8,128)S(1)} %pad_add_fusion), channel_id=1, source_target_pairs={{0,24},{1,25},{2,26},{3,27},{4,28},{5,29},{6,30},{7,31},{8,16},{9,... | collective-permute-start | bytes 196616 | tf_op jit(solution)/shard_map/ppermute | solution.py:66
  6.2 0.8 %collective-permute-start.3 = (f32[8,2048]{1,0:T(8,128)S(1)}, f32[8,2048]{1,0:T(8,128)S(1)}, u32[]{:S(2)}, u32[]{:S(2)}) collective-permute-start(f32[8,2048]{1,0:T(8,128)S(1)} %pad_add_fusion), channel_id=1, source_target_pairs={{0,8},{1,9},{2,10},{3,11},{4,12},{5,13},{6,14},{7,15},{8,24},{9,25... | collective-permute-start | bytes 196616 | tf_op jit(solution)/shard_map/ppermute | solution.py:66
  7.0 1.5 %collective-permute-start = (f32[8,2048]{1,0:T(8,128)S(1)}, f32[8,2048]{1,0:T(8,128)S(1)}, u32[]{:S(2)}, u32[]{:S(2)}) collective-permute-start(f32[8,2048]{1,0:T(8,128)S(1)} %pad_add_fusion), channel_id=1, source_target_pairs={{0,1},{1,0},{2,3},{3,2},{4,5},{5,4},{6,7},{7,6},{8,9},{9,8},{10,11... | collective-permute-start | bytes 196616 | tf_op jit(solution)/shard_map/ppermute | solution.py:66
  8.5 0.0 collective-permute-done.1
  8.5 2.5 %collective-permute-done.2 = f32[8,2048]{1,0:T(8,128)S(1)} collective-permute-done((f32[8,2048]{1,0:T(8,128)S(1)}, f32[8,2048]{1,0:T(8,128)S(1)}, u32[]{:S(2)}, u32[]{:S(2)}) %collective-permute-start.2) | collective-permute-done | bytes 65568 | tf_op jit(solution)/shard_map/ppermute | solution.py:66
  11.0 1.2 %collective-permute-done.3 = f32[8,2048]{1,0:T(8,128)S(1)} collective-permute-done((f32[8,2048]{1,0:T(8,128)S(1)}, f32[8,2048]{1,0:T(8,128)S(1)}, u32[]{:S(2)}, u32[]{:S(2)}) %collective-permute-start.3) | collective-permute-done | bytes 65568 | tf_op jit(solution)/shard_map/ppermute | solution.py:66
  12.3 0.0 copy-start.5
  12.3 0.1 collective-permute-start.4
  12.4 1.6 %collective-permute-start.5 = (f32[16,2048]{1,0:T(8,128)S(1)}, f32[16,2048]{1,0:T(8,128)S(1)}, u32[]{:S(2)}, u32[]{:S(2)}) collective-permute-start(f32[16,2048]{1,0:T(8,128)S(1)} %maximum_select_fusion.rows), channel_id=1, source_target_pairs={{0,6},{1,7},{2,4},{3,5},{4,2},{5,3},{6,0},{7,1},{8,14},{9,15},{10,... | collective-permute-start | bytes 393224 | tf_op jit(solution)/shard_map/ppermute | solution.py:66
  14.0 0.0 copy-start.1
  14.1 0.0 copy-start.2
  14.1 0.0 copy-start.3
  14.1 0.6 %copy-done = f32[512]{0:T(512)S(1)} copy-done((f32[512]{0:T(512)S(1)}, f32[512]{0:T(512)}, u32[]{:S(2)}) %copy-start) | copy-done | bytes 2072
  14.7 0.0 copy-done.2
  14.7 0.0 copy-done.3
  14.8 0.7 %prepare.1 = (f32[2,2048]{1,0:T(2,128)S(1)}, f32[4,128]{1,0:T(4,128)S(1)}, f32[8,128]{1,0:T(8,128)S(1)}, bf16[64,128]{1,0:T(8,128)(2,1)S(1)}) custom-call(f32[2]{0:T(128)S(1)} %copy-done.1, f32[2]{0:T(128)S(1)} %copy-done.2, f32[2]{0:T(128)S(1)} %copy-done.3, f32[1,512]{1,0:T(1,128)S(1)} %bitcast.6, f32[1,1536]{1,0:T(1,128)S(1)} %broadcast_in_dim.7.virtual_energy, ...), custom_call_target="tpu_custom_call" | custom-call | tf_op jit(solution)/shard_map/prepare/pallas_call | solution.py:189
  15.5 2.1 %collective-permute-done.5.rows = f32[16,2048]{1,0:T(8,128)S(1)} collective-permute-done((f32[16,2048]{1,0:T(8,128)S(1)}, f32[16,2048]{1,0:T(8,128)S(1)}, u32[]{:S(2)}, u32[]{:S(2)}) %collective-permute-start.5) | collective-permute-done | bytes 131104 | tf_op jit(solution)/shard_map/ppermute | solution.py:66
  17.6 0.5 %shard_map.83 = f32[32,128]{1,0:T(8,128)S(1)} custom-call(bf16[32,2048]{1,0:T(8,128)(2,1)S(1)} %get-tuple-element.18.left, bf16[32,2048]{1,0:T(8,128)(2,1)S(1)} %get-tuple-element.19.left_low, f32[32,2048]{1,0:T(8,128)S(1)} %pad_maximum_fusion.refs_0_, f32[32,2048]{1,0:T(8,128)S(1)} %collective-permute-done.4.refs_1_, ...), custom_call_target="tpu_custom_call" | custom-call | flops 25165824 | bytes 655360 | tf_op jit(solution)/shard_map/pallas_call | solution.py:216
  18.1 1.6 %collective-permute-start.6 = (f32[32,128]{1,0:T(8,128)S(1)}, f32[32,128]{1,0:T(8,128)S(1)}, u32[]{:S(2)}, u32[]{:S(2)}) collective-permute-start(f32[32,128]{1,0:T(8,128)S(1)} %shard_map.83), channel_id=1, source_target_pairs={{0,6},{1,7},{2,4},{3,5},{4,2},{5,3},{6,0},{7,1},{8,14},{9,15},{10,... | collective-permute-start | bytes 49160 | tf_op jit(solution)/shard_map/ppermute | solution.py:228
  19.8 0.5 %shard_map.82 = f32[32,128]{1,0:T(8,128)S(1)} custom-call(bf16[32,2048]{1,0:T(8,128)(2,1)S(1)} %get-tuple-element.14.left, bf16[32,2048]{1,0:T(8,128)(2,1)S(1)} %get-tuple-element.15.left_low, f32[32,2048]{1,0:T(8,128)S(1)} %pad_maximum_fusion.refs_0_, f32[32,2048]{1,0:T(8,128)S(1)} %collective-permute-done.4.refs_1_, ...), custom_call_target="tpu_custom_call" | custom-call | flops 25165824 | bytes 655360 | tf_op jit(solution)/shard_map/pallas_call | solution.py:216
  20.3 1.0 %collective-permute-done.6 = f32[32,128]{1,0:T(8,128)S(1)} collective-permute-done((f32[32,128]{1,0:T(8,128)S(1)}, f32[32,128]{1,0:T(8,128)S(1)}, u32[]{:S(2)}, u32[]{:S(2)}) %collective-permute-start.6) | collective-permute-done | bytes 16416 | tf_op jit(solution)/shard_map/ppermute | solution.py:228
  21.3 0.6 %add_multiply_fusion = f32[32,128]{1,0:T(8,128)} fusion(f32[32,128]{1,0:T(8,128)S(1)} %shard_map.82, f32[32,128]{1,0:T(8,128)S(1)} %collective-permute-done.6, f32[128]{0:T(128)S(1)} %slice_bitcast_fusion), kind=kLoop, calls=%fused_computation.3 | loop fusion | flops 8192 | bytes 49664 | tf_op jit(solution)/shard_map/mul | solution.py:229
  (13 shorter events, 0.1 us)
Async XLA Ops:
  0.8 7.7 %collective-permute-start.1 = (f32[8,2048]{1,0:T(8,128)S(1)}, f32[8,2048]{1,0:T(8,128)S(1)}, u32[]{:S(2)}, u32[]{:S(2)}) collective-permute-start(f32[8,2048]{1,0:T(8,128)S(1)} %pad_add_fusion), channel_id=1, source_target_pairs={{0,16},{1,17},{2,18},{3,19},{4,20},{5,21},{6,22},{7,23},{8,0},{9,1... | collective-permute-start | bytes 196616 | tf_op jit(solution)/shard_map/ppermute | solution.py:66
  4.9 6.2 %collective-permute-start.2 = (f32[8,2048]{1,0:T(8,128)S(1)}, f32[8,2048]{1,0:T(8,128)S(1)}, u32[]{:S(2)}, u32[]{:S(2)}) collective-permute-start(f32[8,2048]{1,0:T(8,128)S(1)} %pad_add_fusion), channel_id=1, source_target_pairs={{0,24},{1,25},{2,26},{3,27},{4,28},{5,29},{6,30},{7,31},{8,16},{9,... | collective-permute-start | bytes 196616 | tf_op jit(solution)/shard_map/ppermute | solution.py:66
  6.2 6.0 %collective-permute-start.3 = (f32[8,2048]{1,0:T(8,128)S(1)}, f32[8,2048]{1,0:T(8,128)S(1)}, u32[]{:S(2)}, u32[]{:S(2)}) collective-permute-start(f32[8,2048]{1,0:T(8,128)S(1)} %pad_add_fusion), channel_id=1, source_target_pairs={{0,8},{1,9},{2,10},{3,11},{4,12},{5,13},{6,14},{7,15},{8,24},{9,25... | collective-permute-start | bytes 196616 | tf_op jit(solution)/shard_map/ppermute | solution.py:66
  7.0 5.3 %collective-permute-start = (f32[8,2048]{1,0:T(8,128)S(1)}, f32[8,2048]{1,0:T(8,128)S(1)}, u32[]{:S(2)}, u32[]{:S(2)}) collective-permute-start(f32[8,2048]{1,0:T(8,128)S(1)} %pad_add_fusion), channel_id=1, source_target_pairs={{0,1},{1,0},{2,3},{3,2},{4,5},{5,4},{6,7},{7,6},{8,9},{9,8},{10,11... | collective-permute-start | bytes 196616 | tf_op jit(solution)/shard_map/ppermute | solution.py:66
  12.3 1.8 %copy-start.5 = (f32[1536]{0:T(1024)S(1)}, f32[1536]{0:T(1024)}, u32[]{:S(2)}) copy-start(f32[1536]{0:T(1024)} %param.11) | copy-start | bytes 18436
  12.3 5.4 %collective-permute-start.4 = (f32[32,2048]{1,0:T(8,128)S(1)}, f32[32,2048]{1,0:T(8,128)S(1)}, u32[]{:S(2)}, u32[]{:S(2)}) collective-permute-start(f32[32,2048]{1,0:T(8,128)S(1)} %pad_maximum_fusion.refs_0_), channel_id=1, source_target_pairs={{0,2},{1,3},{2,0},{3,1},{4,6},{5,7},{6,4},{7,5},{8,10},{9,11},{10,... | collective-permute-start | bytes 786440 | tf_op jit(solution)/shard_map/ppermute | solution.py:66
  12.4 5.2 %collective-permute-start.5 = (f32[16,2048]{1,0:T(8,128)S(1)}, f32[16,2048]{1,0:T(8,128)S(1)}, u32[]{:S(2)}, u32[]{:S(2)}) collective-permute-start(f32[16,2048]{1,0:T(8,128)S(1)} %maximum_select_fusion.rows), channel_id=1, source_target_pairs={{0,6},{1,7},{2,4},{3,5},{4,2},{5,3},{6,0},{7,1},{8,14},{9,15},{10,... | collective-permute-start | bytes 393224 | tf_op jit(solution)/shard_map/ppermute | solution.py:66
  14.0 0.7 %copy-start = (f32[512]{0:T(512)S(1)}, f32[512]{0:T(512)}, u32[]{:S(2)}) copy-start(f32[512]{0:T(512)} %param.10) | copy-start | bytes 6148
  14.0 0.7 %copy-start.4 = (s32[1,16]{1,0:T(1,128)S(1)}, s32[1,16]{1,0:T(1,128)}, u32[]{:S(2)}) copy-start(s32[1,16]{1,0:T(1,128)} %live.1) | copy-start | bytes 196
  14.0 0.7 %copy-start.1 = (f32[2]{0:T(128)S(1)}, f32[2]{0:T(128)}, u32[]{:S(2)}) copy-start(f32[2]{0:T(128)} %tau.1) | copy-start | bytes 28
  14.1 0.7 %copy-start.2 = (f32[2]{0:T(128)S(1)}, f32[2]{0:T(128)}, u32[]{:S(2)}) copy-start(f32[2]{0:T(128)} %weight.1) | copy-start | bytes 28
  14.1 0.7 %copy-start.3 = (f32[2]{0:T(128)S(1)}, f32[2]{0:T(128)}, u32[]{:S(2)}) copy-start(f32[2]{0:T(128)} %frequency.1) | copy-start | bytes 28
  18.1 3.2 %collective-permute-start.6 = (f32[32,128]{1,0:T(8,128)S(1)}, f32[32,128]{1,0:T(8,128)S(1)}, u32[]{:S(2)}, u32[]{:S(2)}) collective-permute-start(f32[32,128]{1,0:T(8,128)S(1)} %shard_map.83), channel_id=1, source_target_pairs={{0,6},{1,7},{2,4},{3,5},{4,2},{5,3},{6,0},{7,1},{8,14},{9,15},{10,... | collective-permute-start | bytes 49160 | tf_op jit(solution)/shard_map/ppermute | solution.py:228
